TPU v7x, 128 devices: a whole 4x4x4 slice. The times are simulated.
128 devices in a mesh: gx: 8 (over y, core), gy: 16 (over x, z).
Axes of the slice: x: 4, y: 4, z: 4, core: 2. Of those that a mesh axis runs over, the one named last changes fastest.
Arguments:
- old_master: float32 [128, 128, 1536], P('gx', 'gy'), may hold values from -3 to 3
- old_first: float32 [128, 128, 1536], P('gx', 'gy'), may hold values from -3 to 3
- old_second: float32 [128, 128, 1536], P('gx', 'gy'), may hold values from 0.01 to 1
- new_grad: bfloat16 [128, 128, 1536], P(('gx', 'gy')), may hold values from -12288 to 12288
- counts: int32 [128, 128], P(None, ('gx', 'gy')), may hold values from 1 to 72, as said below
- old_owner: int32 [128], replicated, may hold values from 0 to 127, each once
- new_owner: int32 [128], replicated, may hold values from 0 to 127, each once
Outputs:
- new_master: float32 [128, 128, 1536], P(('gx', 'gy'))
- new_first: float32 [128, 128, 1536], P(('gx', 'gy'))
- new_second: float32 [128, 128, 1536], P(('gx', 'gy'))
Inputs may be any that keep to these rules, and one draw needn't show every extreme that they name: `old_owner`: every number of 0 to 127 appears once. `new_owner`: every number of 0 to 127 appears once. `counts`: every device routed at least one token to every expert.
All inputs are finite; a program needn't handle non-finite values.
Results may differ from a plain program's by a relative error of at most 0.0003.
Values sent between devices are 32-bit elements; how exact they have to be, the bound alone decides.
A program may use at most 64 MiB of HBM per device.

v0:
```python
import jax
import jax.numpy as jnp
from jax import lax
from jax.sharding import Mesh
from jax.sharding import PartitionSpec as P

GX = ("gx_0", "gx_1")
GY = ("gy_0", "gy_1")
GX_GY = ("gx_0", "gx_1", "gy_0", "gy_1")


first_correction = 1.0 - 0.9**10
second_correction = 1.0 - 0.999**10


def side_by_side(arrays, axis, split_dim, concat_dim, along):
    ends, at = ([], 0)
    for a in arrays[:-1]:
        at += a.shape[along]
        ends.append(at)
    both = jnp.concatenate(arrays, axis=along)
    return tuple(
        jnp.split(
            lax.all_to_all(both, axis, split_axis=split_dim, concat_axis=concat_dim, tiled=True),
            ends,
            axis=along,
        )
    )


def over_axes(x, axes):
    for axis in axes:
        x = lax.psum(x, axis)
    return x


def adam_step(master, first, second, grad, slot_count):
    scaled = grad.astype(jnp.float32) / slot_count
    new_first = 0.9 * first + 0.1 * scaled
    new_second = 0.999 * second + 0.001 * scaled * scaled
    step_dir = new_first / first_correction / (jnp.sqrt(new_second / second_correction) + 1e-08)
    new_master = master - 0.01 * (step_dir + 0.1 * master)
    return (new_master, new_first, new_second)


def reorder(block, groups_x, groups_y):
    total_rows = block.shape[1]
    piece = total_rows // (groups_x * groups_y)
    shaped = block.reshape(1, groups_x, groups_y, piece, block.shape[2])
    return shaped.transpose(0, 2, 1, 3, 4).reshape(1, total_rows, block.shape[2])


def body(old_master, old_first, old_second, new_grad, counts, old_owner, new_owner):
    experts = old_owner.shape[0]
    groups_x = lax.axis_size(GX)
    groups_y = lax.axis_size(GY)
    my_slot = lax.axis_index(GX) * groups_y + lax.axis_index(GY)
    slots = jnp.arange(experts, dtype=jnp.int32)
    onehot = new_owner[:, None] == slots[None, :]
    source = jnp.sum(jnp.where(onehot, old_owner[:, None], 0), axis=0)
    local_counts = counts[:, 0].astype(jnp.float32)
    by_rows = side_by_side((old_master, old_first, old_second), GX, 1, 0, 2)
    permuted = tuple((jnp.take(state, source, axis=0) for state in by_rows))
    landed = lax.all_to_all(permuted, GX_GY, split_axis=0, concat_axis=1, tiled=True)
    arrived = tuple((reorder(state, groups_x, groups_y) for state in landed))
    totals = over_axes(local_counts, GX_GY)
    slot_count = jnp.sum(jnp.where(new_owner == my_slot, totals, jnp.float32(0.0)))
    return adam_step(arrived[0], arrived[1], arrived[2], new_grad, slot_count)


def solution(mesh):
    torus = Mesh(mesh.devices.reshape(4, 2, 4, 4), ("gx_0", "gx_1", "gy_0", "gy_1"))
    placed = (
        P(GX, GY, None),
        P(GX, GY, None),
        P(GX, GY, None),
        P(GX_GY, None, None),
        P(None, GX_GY),
        P(),
        P(),
    )
    return jax.shard_map(
        body,
        mesh=torus,
        in_specs=placed,
        out_specs=(P(GX_GY, None, None), P(GX_GY, None, None), P(GX_GY, None, None)),
        check_vma=False,
    )
```

profile of v0, /device:TPU:1, one launch (start us, length us, event | category | flops | bytes accessed | tf_op | source)
XLA Modules:
  0.0 143.4 jit_solution(3226954360342858702)
XLA Ops:
  0.6 1.7 %copy.25 = f32[16,8,1536]{2,0,1:T(8,128)S(1)} copy(f32[16,8,1536]{2,1,0:T(8,128)} %param.11) | data formatting | bytes 1572864 | tf_op args[2]
  2.3 1.6 %copy.24 = f32[16,8,1536]{2,0,1:T(8,128)S(1)} copy(f32[16,8,1536]{2,1,0:T(8,128)} %param.10) | data formatting | bytes 1572864 | tf_op args[1]
  4.4 1.6 %pad_maximum_fusion = f32[16,8,4608]{2,0,1:T(8,128)} fusion(f32[16,8,1536]{2,0,1:T(8,128)S(1)} %copy.25, f32[16,8,1536]{2,0,1:T(8,128)S(1)} %copy.24, f32[16,8,1536]{2,0,1:T(8,128)S(1)} %copy.23), kind=kLoop, calls=%fused_computation.3 | loop fusion | flops 1179648 | bytes 4718592 | tf_op jit(solution)/shard_map/concatenate | solution.py:21
  6.0 6.1 %all-to-all-start = ((f32[16,8,4608]{2,0,1:T(8,128)}), f32[16,8,4608]{2,0,1:T(8,128)S(1)}, u32[]{:S(2)}, u32[]{:S(2)}) async-start(f32[16,8,4608]{2,0,1:T(8,128)} %pad_maximum_fusion), calls=%async_computation | async-start | bytes 4718592 | tf_op jit(solution)/shard_map/all_to_all | solution.py:24
  12.2 28.9 %all-to-all-done = f32[16,8,4608]{2,0,1:T(8,128)S(1)} async-done(((f32[16,8,4608]{2,0,1:T(8,128)}), f32[16,8,4608]{2,0,1:T(8,128)S(1)}, u32[]{:S(2)}, u32[]{:S(2)}) %all-to-all-start) | async-done | bytes 2359328 | tf_op jit(solution)/shard_map/all_to_all | solution.py:24
  41.1 1.4 copy-done
  42.5 1.8 %slice_bitcast_fusion = (f32[128,1536]{1,0:T(8,128)S(1)}, f32[128,1536]{1,0:T(8,128)S(1)}, f32[128,1536]{1,0:T(8,128)S(1)}) fusion(f32[128,1,4608]{2,0,1:T(8,128)} %bitcast.43), kind=kLoop, calls=%fused_computation.6 | loop fusion | bytes 4718592 | tf_op jit(solution)/shard_map/jit(_take)/Arg_0.5 | solution.py:63
  44.3 0.9 gather_fusion.2
  45.1 0.9 gather_fusion.1
  46.0 0.9 gather_fusion
  46.9 1.1 bitcast_select_fusion
  48.0 1.7 %copy.28 = f32[128,1,1536]{2,1,0:T(1,128)} copy(f32[128,1,1536]{2,0,1:T(8,128)S(1)} %get-tuple-element.11) | data formatting | bytes 1572864 | tf_op jit(solution)/shard_map/jit(_take)/select_n | solution.py:63
  49.7 8.9 %all-to-all-start.2 = ((f32[128,1,1536]{2,1,0:T(1,128)}), f32[128,1,1536]{2,1,0:T(1,128)S(1)}, u32[]{:S(2)}, u32[]{:S(2)}) async-start(f32[128,1,1536]{2,1,0:T(1,128)} %copy.28), calls=%async_computation.2 | async-start | bytes 1572864 | tf_op jit(solution)/shard_map/all_to_all | solution.py:64
  58.7 1.7 %copy.30 = f32[128,1,1536]{2,1,0:T(1,128)} copy(f32[128,1,1536]{2,0,1:T(8,128)S(1)} %copy-done.1) | data formatting | bytes 1572864 | tf_op jit(solution)/shard_map/jit(_take)/select_n | solution.py:63
  60.4 14.3 %all-to-all-done.2 = f32[128,1,1536]{2,1,0:T(1,128)S(1)} async-done(((f32[128,1,1536]{2,1,0:T(1,128)}), f32[128,1,1536]{2,1,0:T(1,128)S(1)}, u32[]{:S(2)}, u32[]{:S(2)}) %all-to-all-start.2) | async-done | bytes 786464 | tf_op jit(solution)/shard_map/all_to_all | solution.py:64
  74.7 4.8 %all-to-all-start.3 = ((f32[128,1,1536]{2,1,0:T(1,128)}), f32[128,1,1536]{2,1,0:T(1,128)S(1)}, u32[]{:S(2)}, u32[]{:S(2)}) async-start(f32[128,1,1536]{2,1,0:T(1,128)} %copy.30), calls=%async_computation.3 | async-start | bytes 1572864 | tf_op jit(solution)/shard_map/all_to_all | solution.py:64
  79.5 9.5 %psum.28 = f32[128]{0:T(128)S(1)} all-reduce(f32[128]{0:T(128)S(1)} %convert_bitcast_fusion), channel_id=1, replica_groups=mesh['gx_0'=4,'gx_1'=2,'gy_0'=4,'gy_1'=4] {'gx_0'}, use_global_device_ids=true, to_apply=%region_1.3 | all-reduce | flops 128 | bytes 1024 | tf_op jit(solution)/shard_map/psum | solution.py:33
  89.0 4.1 %psum.29 = f32[128]{0:T(128)S(1)} all-reduce(f32[128]{0:T(128)S(1)} %psum.28), channel_id=1, replica_groups=mesh['gx_0'=4,'gx_1'=2,'gy_0'=4,'gy_1'=4] {'gx_1'}, use_global_device_ids=true, to_apply=%region_2.4 | all-reduce | flops 128 | bytes 1024 | tf_op jit(solution)/shard_map/psum | solution.py:33
  93.1 10.9 %psum.30 = f32[128]{0:T(128)S(1)} all-reduce(f32[128]{0:T(128)S(1)} %psum.29), channel_id=1, replica_groups=mesh['gx_0'=4,'gx_1'=2,'gy_0'=4,'gy_1'=4] {'gy_0'}, use_global_device_ids=true, to_apply=%region_3.5 | all-reduce | flops 128 | bytes 1024 | tf_op jit(solution)/shard_map/psum | solution.py:33
  104.1 9.3 %psum.31 = f32[128]{0:T(128)S(1)} all-reduce(f32[128]{0:T(128)S(1)} %psum.30), channel_id=1, replica_groups=mesh['gx_0'=4,'gx_1'=2,'gy_0'=4,'gy_1'=4] {'gy_1'}, use_global_device_ids=true, to_apply=%region_4.6 | all-reduce | flops 128 | bytes 1024 | tf_op jit(solution)/shard_map/psum | solution.py:33
  114.1 1.7 %copy.26 = f32[128,1,1536]{2,1,0:T(1,128)} copy(f32[128,1,1536]{2,0,1:T(8,128)S(1)} %get-tuple-element.12) | data formatting | bytes 1572864 | tf_op jit(solution)/shard_map/jit(_take)/select_n | solution.py:63
  115.8 7.9 %all-to-all-start.1 = ((f32[128,1,1536]{2,1,0:T(1,128)}), f32[128,1,1536]{2,1,0:T(1,128)S(1)}, u32[]{:S(2)}, u32[]{:S(2)}) async-start(f32[128,1,1536]{2,1,0:T(1,128)} %copy.26), calls=%async_computation.1 | async-start | bytes 1572864 | tf_op jit(solution)/shard_map/all_to_all | solution.py:64
  125.4 14.5 %all-to-all-done.1 = f32[128,1,1536]{2,1,0:T(1,128)S(1)} async-done(((f32[128,1,1536]{2,1,0:T(1,128)}), f32[128,1,1536]{2,1,0:T(1,128)S(1)}, u32[]{:S(2)}, u32[]{:S(2)}) %all-to-all-start.1) | async-done | bytes 786464 | tf_op jit(solution)/shard_map/all_to_all | solution.py:64
  139.9 3.5 %bitcast_subtract_fusion = (f32[1,128,1536]{2,1,0:T(8,128)}, f32[1,128,1536]{2,1,0:T(8,128)}, f32[1,128,1536]{2,1,0:T(8,128)}) fusion(f32[1,16,8,1,1536]{4,3,1,2,0:T(1,128)S(1)} %bitcast.44, f32[]{:T(128)} %fusion.3, bf16[1,128,1536]{2,1,0:T(8,128)(2,1)S(1)} %copy-done.3, f32[1,16,8,1,1536]{4,3,1,2,0:T(1,128)S(1)} %bitcast.45, ...), kind=kLoop, calls=%fused_computation.12 | loop fusion | flops 2949120 | bytes 5111812 | tf_op jit(solution)/shard_map/sub | solution.py:42
  (23 shorter events, 2.9 us)
Async XLA Ops:
  0.6 3.3 %copy-start.2 = (f32[16,8,1536]{2,1,0:T(8,128)S(1)}, f32[16,8,1536]{2,1,0:T(8,128)}, u32[]{:S(2)}) copy-start(f32[16,8,1536]{2,1,0:T(8,128)} %param.9) | copy-start | bytes 2359300
  6.0 6.1 %copy-start.4 = (s32[128]{0:T(128)S(1)}, s32[128]{0:T(128)}, u32[]{:S(2)}) copy-start(s32[128]{0:T(128)} %param.15) | copy-start | bytes 1540
  6.0 6.1 %copy-start.5 = (s32[128]{0:T(128)S(1)}, s32[128]{0:T(128)}, u32[]{:S(2)}) copy-start(s32[128]{0:T(128)} %param.14) | copy-start | bytes 1540
  6.0 35.1 %all-to-all-start = ((f32[16,8,4608]{2,0,1:T(8,128)}), f32[16,8,4608]{2,0,1:T(8,128)S(1)}, u32[]{:S(2)}, u32[]{:S(2)}) async-start(f32[16,8,4608]{2,0,1:T(8,128)} %pad_maximum_fusion), calls=%async_computation | async-start | bytes 4718592 | tf_op jit(solution)/shard_map/all_to_all | solution.py:24
  41.1 1.4 copy-start
  48.0 10.6 %copy-start.1 = (f32[128,1,1536]{2,0,1:T(8,128)S(1)}, f32[128,1,1536]{2,0,1:T(8,128)}, u32[]{:S(2)}) copy-start(f32[128,1,1536]{2,0,1:T(8,128)} %get-tuple-element.10) | copy-start | bytes 2359300
  49.7 29.8 %copy-start.6 = (s32[128,1]{0,1:T(1,128)S(1)}, s32[128,1]{0,1:T(1,128)}, u32[]{:S(2)}) copy-start(s32[128,1]{0,1:T(1,128)} %param.13) | copy-start | bytes 1540
  49.7 25.0 %all-to-all-start.2 = ((f32[128,1,1536]{2,1,0:T(1,128)}), f32[128,1,1536]{2,1,0:T(1,128)S(1)}, u32[]{:S(2)}, u32[]{:S(2)}) async-start(f32[128,1,1536]{2,1,0:T(1,128)} %copy.28), calls=%async_computation.2 | async-start | bytes 1572864 | tf_op jit(solution)/shard_map/all_to_all | solution.py:64
  74.7 41.1 %all-to-all-start.3 = ((f32[128,1,1536]{2,1,0:T(1,128)}), f32[128,1,1536]{2,1,0:T(1,128)S(1)}, u32[]{:S(2)}, u32[]{:S(2)}) async-start(f32[128,1,1536]{2,1,0:T(1,128)} %copy.30), calls=%async_computation.3 | async-start | bytes 1572864 | tf_op jit(solution)/shard_map/all_to_all | solution.py:64
  115.8 24.1 %copy-start.3 = (bf16[1,128,1536]{2,1,0:T(8,128)(2,1)S(1)}, bf16[1,128,1536]{2,1,0:T(8,128)(2,1)}, u32[]{:S(2)}) copy-start(bf16[1,128,1536]{2,1,0:T(8,128)(2,1)} %param.12) | copy-start | bytes 1179652
  115.8 24.1 %all-to-all-start.1 = ((f32[128,1,1536]{2,1,0:T(1,128)}), f32[128,1,1536]{2,1,0:T(1,128)S(1)}, u32[]{:S(2)}, u32[]{:S(2)}) async-start(f32[128,1,1536]{2,1,0:T(1,128)} %copy.26), calls=%async_computation.1 | async-start | bytes 1572864 | tf_op jit(solution)/shard_map/all_to_all | solution.py:64
where the time goes:
time: 144 us; the launch traced here: 143 us
  waiting for transfers between devices  57.7 us (40%)
  blocking collectives  33.9 us (24%)
  starting transfers between devices  27.7 us (19%)
  local copies, waits for them, and re-layouts  14.6 us (10%)
  other arithmetic  8.7 us (6%)
    psum x4, blocking collectives, over_axes(): x = lax.psum(x, axis)  33.9 us
    all_to_all x1, waiting for transfers between devices, side_by_side(): lax.all_to_all(both, axis, split_axis=split_dim, concat_axis=concat_dim,...  28.9 us
    all_to_all x3, waiting for transfers between devices, body(): lax.all_to_all(permuted, GX_GY, split_axis=0, concat_axis=1, tiled=True)  28.8 us
    all_to_all x3, starting transfers between devices, body(): lax.all_to_all(permuted, GX_GY, split_axis=0, concat_axis=1, tiled=True)  21.7 us
    all_to_all x1, starting transfers between devices, side_by_side(): lax.all_to_all(both, axis, split_axis=split_dim, concat_axis=concat_dim,...  6.09 us
    unnamed x17, local copies, waits for them, and re-layouts  5.16 us
    select_n x3, local copies, waits for them, and re-layouts, body(): permuted = tuple((jnp.take(state, source, axis=0) for state in by_rows))  5.06 us
    sub x1, other arithmetic, adam_step(): new_master = master - 0.01 * (step_dir + 0.1 * master)  3.52 us
  transfers between devices with their start and end apart: 4, of which 3 were waited for; matrix products, arithmetic and copies ran while one was open for 4% of the time, Pallas kernels for 0%

commit v1 on v0

v1 whole, which is shorter than its diff:
```python
import functools

import jax
import jax.numpy as jnp
from jax import lax
from jax.experimental import pallas as pl
from jax.experimental.pallas import tpu as pltpu
from jax.sharding import PartitionSpec as P

MESH = pl.DeviceIdType.MESH
LANES = 128
ORDER = (1, 3, 2)
Z_LAG = 2
Y_LAG = 4

first_correction = 1.0 - 0.9**10
second_correction = 1.0 - 0.999**10


def device(x, y, z, c):
    return (y * 2 + c, x * 4 + z)


def mod4(v):
    return lax.rem(v + 4, 4)


def exchange_kernel(
    chunks, third, source_ref, counts_ref, *refs
):
    states, (outs, totals_ref), scratch = refs[:3], (refs[3:6], refs[6]), refs[7:]
    n = len(chunks)
    a_bufs, b_bufs, c_bufs, d_bufs = (scratch[i * n : (i + 1) * n] for i in range(4))
    count_g, count_x, count_z, sx, sz = scratch[4 * n : 4 * n + 5]
    sems = scratch[4 * n + 5 :]
    y1_send, y1_recv, own_sem, core_send, core_recv, x_send, x_recv = sems[:7]
    z_send, z_recv, y2_send, y2_recv, out_sem, n_send, n_recv = sems[7:]

    gx, gy = lax.axis_index("gx"), lax.axis_index("gy")
    x, y, z, c = lax.div(gy, 4), lax.div(gx, 2), lax.rem(gy, 4), lax.rem(gx, 2)
    other = 1 - c

    xs = [device(mod4(x + d), y, z, c) for d in range(4)]
    ys = [device(x, mod4(y + d), z, c) for d in range(4)]
    zs = [device(x, y, mod4(z + d), c) for d in range(4)]
    gs = [(lax.rem(gx + d, 8), gy) for d in range(8)]

    barrier = pltpu.get_barrier_semaphore()
    for peer in gs[1:] + xs[1:] + zs[1:]:
        pl.semaphore_signal(barrier, inc=1, device_id=peer, device_id_type=MESH)
    pl.semaphore_wait(barrier, 13)

    started = []

    def remote(src, dst, send, recv, peer):
        copy = pltpu.make_async_remote_copy(
            src_ref=src, dst_ref=dst, send_sem=send, recv_sem=recv, device_id=peer, device_id_type=MESH
        )
        copy.start()
        started.append(copy)
        return copy

    def block(owner_y, owner_c):
        return pl.ds(pl.multiple_of((owner_y * 2 + owner_c) * 16, 16), 16)

    def columns(owner_y, offset, width):
        return pl.ds(pl.multiple_of(owner_y * third + offset, LANES), width)

    count_g[pl.ds(gx, 1)] = counts_ref[...].reshape(1, 1, LANES)
    y1, own, cores = [], [], []
    for k, (s, offset, width) in enumerate(chunks):
        y1.append(
            {
                d: remote(
                    states[s].at[:, :, columns(mod4(y + d), offset, width)],
                    a_bufs[k].at[block(y, c)],
                    y1_send.at[k, d],
                    y1_recv.at[k, d],
                    ys[d],
                )
                for d in ORDER
            }
        )
        mine = states[s].at[:, :, columns(y, offset, width)]
        local = pltpu.make_async_copy(mine, a_bufs[k].at[block(y, c)], own_sem.at[k])
        local.start()
        own.append(local)
        cores.append(
            {0: remote(mine, a_bufs[k].at[block(y, c)], core_send.at[k, 0], core_recv.at[k, 0], gs_partner(x, y, z, other))}
        )
        if k == 0:
            tallies = [
                remote(counts_ref, count_g.at[gx], n_send.at[d], n_recv.at[d], gs[d]) for d in range(1, 8)
            ]

    def forward(k):
        for d in ORDER:
            y1[k][d].wait_recv()
            held = a_bufs[k].at[block(mod4(y - d), c)]
            cores[k][d] = remote(held, held, core_send.at[k, d], core_recv.at[k, d], gs_partner(x, y, z, other))

    sent_x, sent_z, sent_y = {}, {}, {}

    def permute(k):
        own[k].wait()
        for d in range(4):
            cores[k][d].wait_recv()
        for d in range(4):
            base = 4 * mod4(x + d) + 16 * c

            def place(j, carry, d=d, base=base):
                to_z, to_y = lax.div(j, 4), lax.rem(j, 4)
                tile = a_bufs[k][source_ref[base + 32 * to_y + to_z]]
                if d == 0:
                    c_bufs[k][x, to_z, to_y] = tile
                else:
                    b_bufs[k][d - 1, to_z, to_y] = tile
                return carry

            lax.fori_loop(0, 16, place, 0, unroll=4)
        sent_x[k] = [
            remote(b_bufs[k].at[d - 1], c_bufs[k].at[x], x_send.at[k, d], x_recv.at[k, d], xs[d]) for d in ORDER
        ]

    def along_z(k):
        for copy in sent_x[k]:
            copy.wait_recv()
        sent_z[k] = [
            remote(
                c_bufs[k].at[:, mod4(z + d)], d_bufs[k].at[:, z], z_send.at[k, d], z_recv.at[k, d], zs[d]
            )
            for d in ORDER
        ]
        d_bufs[k][:, pl.ds(z, 1)] = c_bufs[k][:, pl.ds(z, 1)]

    def along_y(k):
        s, offset, width = chunks[k]
        for copy in sent_z[k]:
            copy.wait_recv()
        landing = outs[s].at[:, :, :, columns(y, offset, width)]
        sent_y[k] = [
            remote(d_bufs[k].at[:, :, mod4(y + d)], landing, y2_send.at[k, d], y2_recv.at[k, d], ys[d])
            for d in ORDER
        ]
        local = pltpu.make_async_copy(d_bufs[k].at[:, :, y], landing, out_sem.at[k])
        local.start()
        own[k] = local

    def tally_x():
        for copy in tallies:
            copy.wait_recv()
        count = jnp.sum(count_g[...], axis=0)
        sx[...] = count
        count_x[pl.ds(x, 1)] = count.reshape(1, 1, LANES)

    def tally_send_x():
        return [
            remote(sx, count_x.at[x], n_send.at[7 + d], n_recv.at[7 + d], xs[d]) for d in range(1, 4)
        ]

    def tally_z(copies):
        for copy in copies:
            copy.wait_recv()
        count = jnp.sum(count_x[...], axis=0)
        sz[...] = count
        count_z[pl.ds(z, 1)] = count.reshape(1, 1, LANES)

    def tally_send_z():
        return [
            remote(sz, count_z.at[z], n_send.at[10 + d], n_recv.at[10 + d], zs[d]) for d in range(1, 4)
        ]

    counted = None
    for i in range(n + Y_LAG):
        if i < n:
            forward(i)
        if 0 <= i - Y_LAG < n:
            along_y(i - Y_LAG)
        if 0 <= i - Z_LAG < n:
            along_z(i - Z_LAG)
        if i == 1:
            counted = tally_send_x()
        if i == 4:
            counted = tally_send_z()
        if i < n:
            permute(i)
        if i == 0:
            tally_x()
        if i == 3:
            tally_z(counted)
    for copy in counted:
        copy.wait_recv()
    totals_ref[...] = jnp.sum(count_z[...], axis=0)
    for k in range(n):
        own[k].wait()
        for copy in sent_y[k]:
            copy.wait_recv()
    for copy in started:
        copy.wait_send()


def gs_partner(x, y, z, other):
    return device(x, y, z, other)


def adam_step(master, first, second, grad, slot_count):
    scaled = grad.astype(jnp.float32) / slot_count
    new_first = 0.9 * first + 0.1 * scaled
    new_second = 0.999 * second + 0.001 * scaled * scaled
    step_dir = new_first / first_correction / (jnp.sqrt(new_second / second_correction) + 1e-08)
    new_master = master - 0.01 * (step_dir + 0.1 * master)
    return (new_master, new_first, new_second)


def body(old_master, old_first, old_second, new_grad, counts, old_owner, new_owner):
    experts = old_owner.shape[0]
    group, rows, ff = old_master.shape
    third = ff // 4
    my_slot = lax.axis_index("gx") * lax.axis_size("gy") + lax.axis_index("gy")
    slots = jnp.arange(experts, dtype=jnp.int32)
    onehot = new_owner[:, None] == slots[None, :]
    source = jnp.sum(jnp.where(onehot, old_owner[:, None], 0), axis=0)
    local_counts = counts.astype(jnp.float32).reshape(1, experts)

    chunks = [(s, offset, LANES) for s in range(3) for offset in range(0, third, LANES)]
    n = len(chunks)
    f32 = jnp.float32
    dma = pltpu.SemaphoreType.DMA
    scratch = (
        [pltpu.VMEM((experts, rows, w), f32) for _, _, w in chunks]
        + [pltpu.VMEM((3, 4, 4, rows, w), f32) for _, _, w in chunks]
        + [pltpu.VMEM((4, 4, 4, rows, w), f32) for _, _, w in chunks]
        + [pltpu.VMEM((4, 4, 4, rows, w), f32) for _, _, w in chunks]
        + [pltpu.VMEM((8, 1, experts), f32), pltpu.VMEM((4, 1, experts), f32), pltpu.VMEM((4, 1, experts), f32)]
        + [pltpu.VMEM((1, experts), f32), pltpu.VMEM((1, experts), f32)]
        + [dma((n, 4)), dma((n, 4)), dma((n,)), dma((n, 4)), dma((n, 4)), dma((n, 4)), dma((n, 4))]
        + [dma((n, 4)), dma((n, 4)), dma((n, 4)), dma((n, 4)), dma((n,)), dma((14,)), dma((14,))]
    )
    landed = jax.ShapeDtypeStruct((4, 4, rows, ff), f32)
    vmem, hbm = pl.BlockSpec(memory_space=pltpu.VMEM), pl.BlockSpec(memory_space=pl.ANY)
    master, first, second, totals = pl.pallas_call(
        functools.partial(exchange_kernel, chunks, third),
        name="exchange",
        out_shape=(landed, landed, landed, jax.ShapeDtypeStruct((1, experts), f32)),
        in_specs=[pl.BlockSpec(memory_space=pltpu.SMEM), vmem, hbm, hbm, hbm],
        out_specs=(hbm, hbm, hbm, vmem),
        scratch_shapes=scratch,
        compiler_params=pltpu.CompilerParams(
            collective_id=0, has_side_effects=True, vmem_limit_bytes=60 * 1024 * 1024
        ),
    )(source, local_counts, old_master, old_first, old_second)
    shape = (1, 16 * rows, ff)
    slot_count = jnp.sum(jnp.where(new_owner == my_slot, totals[0], jnp.float32(0.0)))
    return adam_step(master.reshape(shape), first.reshape(shape), second.reshape(shape), new_grad, slot_count)


def solution(mesh):
    placed = (
        P("gx", "gy", None),
        P("gx", "gy", None),
        P("gx", "gy", None),
        P(("gx", "gy"), None, None),
        P(None, ("gx", "gy")),
        P(),
        P(),
    )
    out = P(("gx", "gy"), None, None)
    return jax.shard_map(body, mesh=mesh, in_specs=placed, out_specs=(out, out, out), check_vma=False)
```

time: 144 us -> 71.9 us (0.50)
  Pallas kernels: 0 us -> 63.4 us
  waiting for transfers between devices: 57.7 us -> 0 us
  blocking collectives: 33.9 us -> 0 us
  starting transfers between devices: 27.7 us -> 0 us
  local copies, waits for them, and re-layouts: 14.6 us -> 1.48 us
  other arithmetic: 8.7 us -> 5.69 us
    pallas_call x0 -> x1, Pallas kernels: none -> 63.4 us  [body(): pl.pallas_call(functools.partial(exchange_kernel, chunks, third), name='e...]
    all_to_all x4 -> x0, waiting for transfers between devices: 57.7 us -> none  [the longest x1 28.9 us: side_by_side(): lax.all_to_all(both, axis, split_axis=split_dim, concat_axis=concat_dim,...]
    psum x4 -> x0, blocking collectives: 33.9 us -> none  [over_axes(): x = lax.psum(x, axis)]
    all_to_all x4 -> x0, starting transfers between devices: 27.7 us -> none  [the longest x3 21.7 us: body(): lax.all_to_all(permuted, GX_GY, split_axis=0, concat_axis=1, tiled=True)]
    select_n x3 -> x0, local copies, waits for them, and re-layouts: 5.06 us -> none  [body(): permuted = tuple((jnp.take(state, source, axis=0) for state in by_rows))]
    unnamed x17 -> x12, local copies, waits for them, and re-layouts: 5.16 us -> 1.48 us
    gather x3 -> x0, local copies, waits for them, and re-layouts: 2.63 us -> none  [body(): permuted = tuple((jnp.take(state, source, axis=0) for state in by_rows))]
    another operation x1 -> x0, local copies, waits for them, and re-layouts: 1.76 us -> none  [body(): permuted = tuple((jnp.take(state, source, axis=0) for state in by_rows))]
  transfers between devices with their start and end apart: 4 -> 0, of which waited for: 3 -> 0; matrix products, arithmetic and copies ran while one was open for 4% -> 0% of each run, Pallas kernels for 0% -> 0%
where the time goes in v1:
time: 71.9 us; the launch traced here: 71.2 us
  Pallas kernels  63.4 us (88%)
  other arithmetic  5.69 us (8%)
  local copies, waits for them, and re-layouts  1.48 us (2%)
    pallas_call x1, Pallas kernels, body(): pl.pallas_call(functools.partial(exchange_kernel, chunks, third), name='e...  63.4 us
    sub x1, other arithmetic, adam_step(): new_master = master - 0.01 * (step_dir + 0.1 * master)  2.34 us
    mul x1, other arithmetic, adam_step(): new_second = 0.999 * second + 0.001 * scaled * scaled  1.61 us
    unnamed x12, local copies, waits for them, and re-layouts  1.48 us

profile of v1, /device:TPU:1, one launch (start us, length us, event | category | flops | bytes accessed | tf_op | source)
XLA Modules:
  0.0 71.2 jit_solution(11984519311389124722)
XLA Ops:
  0.6 0.0 copy-start.4
  0.6 0.6 copy-done.4
  1.3 0.0 copy-start.2
  1.3 0.0 copy-start.5
  1.3 0.5 convert_bitcast_fusion.counts_ref
  1.8 0.1 copy-done.2
  2.0 0.0 copy-done.5
  2.0 0.6 select_reduce_fusion.source_ref
  2.6 63.4 %exchange.1 = (f32[4,4,8,1536]{3,2,1,0:T(8,128)}, f32[4,4,8,1536]{3,2,1,0:T(8,128)}, f32[4,4,8,1536]{3,2,1,0:T(8,128)}, f32[1,128]{1,0:T(1,128)}) custom-call(s32[128]{0:T(128)} %select_reduce_fusion.source_ref, f32[1,128]{1,0:T(1,128)} %convert_bitcast_fusion.counts_ref, f32[16,8,1536]{2,1,0:T(8,128)} %refs_0_.1, f32[16,8,1536]{2,1,0:T(8,128)} %refs_1_.1, ...), custom_call_target="tpu_custom_call" | custom-call | tf_op jit(solution)/shard_map/exchange/pallas_call | solution.py:241
  66.0 0.0 copy-start.3
  66.0 0.6 copy-done.3
  66.6 0.6 fusion.1
  67.2 0.0 copy-start
  67.2 0.0 copy-start.1
  67.2 1.6 %broadcast_multiply_fusion = (f32[4,4,8,1536]{3,2,1,0:T(8,128)S(1)}, f32[4,4,8,1536]{3,2,1,0:T(8,128)S(1)}) fusion(f32[4,4,8,1536]{3,2,1,0:T(8,128)} %get-tuple-element.10, f32[4,4,8,1536]{3,2,1,0:T(8,128)} %get-tuple-element.8), kind=kLoop, calls=%fused_computation.5 | loop fusion | flops 393216 | bytes 3145728 | tf_op jit(solution)/shard_map/mul | solution.py:209
  68.8 0.0 copy-done
  68.8 0.1 copy-done.1
  68.9 2.3 %multiply_subtract_fusion = (f32[1,128,1536]{2,1,0:T(8,128)}, f32[1,128,1536]{2,1,0:T(8,128)}, f32[1,128,1536]{2,1,0:T(8,128)}) fusion(f32[1,128,1536]{2,1,0:T(8,128)S(1)} %bitcast.9, f32[1,128,1536]{2,1,0:T(8,128)S(1)} %bitcast.8, f32[]{:T(128)} %fusion.1, bf16[1,128,1536]{2,1,0:T(8,128)(2,1)S(1)} %copy-done.1, f32[1,128,1536]{2,1,0:T(8,128)S(1)} %bitcast.7), kind=kLoop, calls=%fused_computation.2 | loop fusion | flops 2949120 | bytes 5111812 | tf_op jit(solution)/shard_map/sub | solution.py:211
Async XLA Ops:
  0.6 0.7 copy-start.4
  1.3 0.7 copy-start.2
  1.3 0.7 copy-start.5
  66.0 0.6 copy-start.3
  67.2 1.6 %copy-start = (f32[4,4,8,1536]{3,2,1,0:T(8,128)S(1)}, f32[4,4,8,1536]{3,2,1,0:T(8,128)}, u32[]{:S(2)}) copy-start(f32[4,4,8,1536]{3,2,1,0:T(8,128)} %get-tuple-element.7) | copy-start | bytes 2359300
  67.2 1.7 %copy-start.1 = (bf16[1,128,1536]{2,1,0:T(8,128)(2,1)S(1)}, bf16[1,128,1536]{2,1,0:T(8,128)(2,1)}, u32[]{:S(2)}) copy-start(bf16[1,128,1536]{2,1,0:T(8,128)(2,1)} %param.10) | copy-start | bytes 1179652

commit v2 on v1

--- a/solution.py
+++ b/solution.py
@@ -12,6 +12,7 @@
 ORDER = (1, 3, 2)
 Z_LAG = 2
 Y_LAG = 4
+ADAM_ROWS = 32
 
 first_correction = 1.0 - 0.9**10
 second_correction = 1.0 - 0.999**10
@@ -26,15 +27,15 @@
 
 
 def exchange_kernel(
-    chunks, third, source_ref, counts_ref, *refs
+    chunks, quarter, counts_ref, old_owner_ref, new_owner_ref, *refs
 ):
-    states, (outs, totals_ref), scratch = refs[:3], (refs[3:6], refs[6]), refs[7:]
+    states, (outs, slot_count_ref), scratch = refs[:3], (refs[3:6], refs[6]), refs[7:]
     n = len(chunks)
     a_bufs, b_bufs, c_bufs, d_bufs = (scratch[i * n : (i + 1) * n] for i in range(4))
-    count_g, count_x, count_z, sx, sz = scratch[4 * n : 4 * n + 5]
-    sems = scratch[4 * n + 5 :]
+    count_g, count_x, count_z, sx, sz, owners, source_row, source_ref = scratch[4 * n : 4 * n + 8]
+    sems = scratch[4 * n + 8 :]
     y1_send, y1_recv, own_sem, core_send, core_recv, x_send, x_recv = sems[:7]
-    z_send, z_recv, y2_send, y2_recv, out_sem, n_send, n_recv = sems[7:]
+    z_send, z_recv, y2_send, y2_recv, out_sem, n_send, n_recv, small_sem = sems[7:]
 
     gx, gy = lax.axis_index("gx"), lax.axis_index("gy")
     x, y, z, c = lax.div(gy, 4), lax.div(gx, 2), lax.rem(gy, 4), lax.rem(gx, 2)
@@ -64,9 +65,15 @@
         return pl.ds(pl.multiple_of((owner_y * 2 + owner_c) * 16, 16), 16)
 
     def columns(owner_y, offset, width):
-        return pl.ds(pl.multiple_of(owner_y * third + offset, LANES), width)
-
-    count_g[pl.ds(gx, 1)] = counts_ref[...].reshape(1, 1, LANES)
+        return pl.ds(pl.multiple_of(owner_y * quarter + offset, LANES), width)
+
+    small = [
+        pltpu.make_async_copy(old_owner_ref, owners.at[0], small_sem.at[0]),
+        pltpu.make_async_copy(new_owner_ref, owners.at[1], small_sem.at[1]),
+        pltpu.make_async_copy(counts_ref, count_g.at[gx], small_sem.at[2]),
+    ]
+    for copy in small:
+        copy.start()
     y1, own, cores = [], [], []
     for k, (s, offset, width) in enumerate(chunks):
         y1.append(
@@ -93,6 +100,15 @@
                 remote(counts_ref, count_g.at[gx], n_send.at[d], n_recv.at[d], gs[d]) for d in range(1, 8)
             ]
 
+    for copy in small:
+        copy.wait()
+    old_column = jnp.broadcast_to(owners[0], (LANES, LANES)).T
+    new_column = jnp.broadcast_to(owners[1], (LANES, LANES)).T
+    lanes = lax.broadcasted_iota(jnp.int32, (LANES, LANES), 1)
+    source_row[...] = jnp.sum(jnp.where(new_column == lanes, old_column, 0), axis=0, keepdims=True)
+    to_scalar = pltpu.make_async_copy(source_row, source_ref, small_sem.at[3])
+    to_scalar.start()
+
     def forward(k):
         for d in ORDER:
             y1[k][d].wait_recv()
@@ -110,7 +126,7 @@
 
             def place(j, carry, d=d, base=base):
                 to_z, to_y = lax.div(j, 4), lax.rem(j, 4)
-                tile = a_bufs[k][source_ref[base + 32 * to_y + to_z]]
+                tile = a_bufs[k][source_ref[0, base + 32 * to_y + to_z]]
                 if d == 0:
                     c_bufs[k][x, to_z, to_y] = tile
                 else:
@@ -149,7 +165,7 @@
     def tally_x():
         for copy in tallies:
             copy.wait_recv()
-        count = jnp.sum(count_g[...], axis=0)
+        count = jnp.sum(count_g[...].astype(jnp.float32), axis=0)
         sx[...] = count
         count_x[pl.ds(x, 1)] = count.reshape(1, 1, LANES)
 
@@ -182,6 +198,8 @@
             counted = tally_send_x()
         if i == 4:
             counted = tally_send_z()
+        if i == 0:
+            to_scalar.wait()
         if i < n:
             permute(i)
         if i == 0:
@@ -190,7 +208,9 @@
             tally_z(counted)
     for copy in counted:
         copy.wait_recv()
-    totals_ref[...] = jnp.sum(count_z[...], axis=0)
+    totals = jnp.sum(count_z[...], axis=0)
+    mine = jnp.where(owners[1] == gx * 16 + gy, totals, 0.0)
+    slot_count_ref[...] = jnp.broadcast_to(jnp.sum(mine, axis=1, keepdims=True), (1, LANES))
     for k in range(n):
         own[k].wait()
         for copy in sent_y[k]:
@@ -203,26 +223,37 @@
     return device(x, y, z, other)
 
 
-def adam_step(master, first, second, grad, slot_count):
-    scaled = grad.astype(jnp.float32) / slot_count
-    new_first = 0.9 * first + 0.1 * scaled
-    new_second = 0.999 * second + 0.001 * scaled * scaled
-    step_dir = new_first / first_correction / (jnp.sqrt(new_second / second_correction) + 1e-08)
-    new_master = master - 0.01 * (step_dir + 0.1 * master)
-    return (new_master, new_first, new_second)
+def adam_kernel(slot_count, master, first, second, grad, new_master, new_first, new_second):
+    scaled = grad[0].astype(jnp.float32) / slot_count[0:1, 0:1]
+    moved_first = 0.9 * first[0] + 0.1 * scaled
+    moved_second = 0.999 * second[0] + 0.001 * scaled * scaled
+    step_dir = moved_first / first_correction / (jnp.sqrt(moved_second / second_correction) + 1e-08)
+    new_master[0] = master[0] - 0.01 * (step_dir + 0.1 * master[0])
+    new_first[0] = moved_first
+    new_second[0] = moved_second
+
+
+def adam_step(master, first, second, grad, slot_count, block_rows=ADAM_ROWS):
+    _, rows, ff = grad.shape
+    tile = pl.BlockSpec((1, block_rows, ff), lambda i: (0, i, 0))
+    state = jax.ShapeDtypeStruct((1, rows, ff), jnp.float32)
+    return pl.pallas_call(
+        adam_kernel,
+        name="adam",
+        grid=(rows // block_rows,),
+        out_shape=(state, state, state),
+        in_specs=[pl.BlockSpec((1, LANES), lambda i: (0, 0)), tile, tile, tile, tile],
+        out_specs=(tile, tile, tile),
+    )(slot_count, master, first, second, grad)
 
 
 def body(old_master, old_first, old_second, new_grad, counts, old_owner, new_owner):
     experts = old_owner.shape[0]
     group, rows, ff = old_master.shape
-    third = ff // 4
-    my_slot = lax.axis_index("gx") * lax.axis_size("gy") + lax.axis_index("gy")
-    slots = jnp.arange(experts, dtype=jnp.int32)
-    onehot = new_owner[:, None] == slots[None, :]
-    source = jnp.sum(jnp.where(onehot, old_owner[:, None], 0), axis=0)
-    local_counts = counts.astype(jnp.float32).reshape(1, experts)
-
-    chunks = [(s, offset, LANES) for s in range(3) for offset in range(0, third, LANES)]
+    quarter = ff // 4
+    row = (1, experts)
+
+    chunks = [(s, offset, LANES) for s in range(3) for offset in range(0, quarter, LANES)]
     n = len(chunks)
     f32 = jnp.float32
     dma = pltpu.SemaphoreType.DMA
@@ -231,26 +262,26 @@
         + [pltpu.VMEM((3, 4, 4, rows, w), f32) for _, _, w in chunks]
         + [pltpu.VMEM((4, 4, 4, rows, w), f32) for _, _, w in chunks]
         + [pltpu.VMEM((4, 4, 4, rows, w), f32) for _, _, w in chunks]
-        + [pltpu.VMEM((8, 1, experts), f32), pltpu.VMEM((4, 1, experts), f32), pltpu.VMEM((4, 1, experts), f32)]
-        + [pltpu.VMEM((1, experts), f32), pltpu.VMEM((1, experts), f32)]
+        + [pltpu.VMEM((8, 1, experts), jnp.int32), pltpu.VMEM((4, 1, experts), f32), pltpu.VMEM((4, 1, experts), f32)]
+        + [pltpu.VMEM((1, experts), f32), pltpu.VMEM((1, experts), f32), pltpu.VMEM((2, 1, experts), jnp.int32)]
+        + [pltpu.VMEM((1, experts), jnp.int32), pltpu.SMEM((1, experts), jnp.int32)]
         + [dma((n, 4)), dma((n, 4)), dma((n,)), dma((n, 4)), dma((n, 4)), dma((n, 4)), dma((n, 4))]
-        + [dma((n, 4)), dma((n, 4)), dma((n, 4)), dma((n, 4)), dma((n,)), dma((14,)), dma((14,))]
+        + [dma((n, 4)), dma((n, 4)), dma((n, 4)), dma((n, 4)), dma((n,)), dma((14,)), dma((14,)), dma((4,))]
     )
     landed = jax.ShapeDtypeStruct((4, 4, rows, ff), f32)
     vmem, hbm = pl.BlockSpec(memory_space=pltpu.VMEM), pl.BlockSpec(memory_space=pl.ANY)
-    master, first, second, totals = pl.pallas_call(
-        functools.partial(exchange_kernel, chunks, third),
+    master, first, second, slot_count = pl.pallas_call(
+        functools.partial(exchange_kernel, chunks, quarter),
         name="exchange",
         out_shape=(landed, landed, landed, jax.ShapeDtypeStruct((1, experts), f32)),
-        in_specs=[pl.BlockSpec(memory_space=pltpu.SMEM), vmem, hbm, hbm, hbm],
+        in_specs=[hbm] * 6,
         out_specs=(hbm, hbm, hbm, vmem),
         scratch_shapes=scratch,
         compiler_params=pltpu.CompilerParams(
             collective_id=0, has_side_effects=True, vmem_limit_bytes=60 * 1024 * 1024
         ),
-    )(source, local_counts, old_master, old_first, old_second)
+    )(counts.reshape(row), old_owner.reshape(row), new_owner.reshape(row), old_master, old_first, old_second)
     shape = (1, 16 * rows, ff)
-    slot_count = jnp.sum(jnp.where(new_owner == my_slot, totals[0], jnp.float32(0.0)))
     return adam_step(master.reshape(shape), first.reshape(shape), second.reshape(shape), new_grad, slot_count)
 
 

time: 71.9 us -> 68.5 us (0.953)
  other arithmetic: 5.69 us -> 0 us
  Pallas kernels: 63.4 us -> 67.2 us
  local copies, waits for them, and re-layouts: 1.48 us -> 0 us
    pallas_call x1 -> x2, Pallas kernels: 63.4 us -> 67.2 us  [the longest x1 62.9 us: body(): pl.pallas_call(functools.partial(exchange_kernel, chunks, quarter), name=...]
    sub x1 -> x0, other arithmetic: 2.34 us -> none  [adam_step(): new_master = master - 0.01 * (step_dir + 0.1 * master)]
    mul x1 -> x0, other arithmetic: 1.61 us -> none  [adam_step(): new_second = 0.999 * second + 0.001 * scaled * scaled]
    unnamed x12 -> x0, local copies, waits for them, and re-layouts: 1.48 us -> none
    reduce_sum x2 -> x0, other arithmetic: 1.22 us -> none  [the longest x1 0.62 us: body(): source = jnp.sum(jnp.where(onehot, old_owner[:, None], 0), axis=0)]
where the time goes in v2:
time: 68.5 us; the launch traced here: 67.9 us
  Pallas kernels  67.2 us (98%)
    pallas_call x1, Pallas kernels, body(): pl.pallas_call(functools.partial(exchange_kernel, chunks, quarter), name=...  62.9 us
    pallas_call x1, Pallas kernels, adam_step(): pl.pallas_call(adam_kernel, name='adam', grid=(rows // block_rows,), out_...  4.36 us

profile of v2, /device:TPU:1, one launch (start us, length us, event | category | flops | bytes accessed | tf_op | source)
XLA Modules:
  0.0 67.9 jit_solution(16944515262784017604)
XLA Ops:
  0.6 62.9 %exchange.1 = (f32[4,4,8,1536]{3,2,1,0:T(8,128)}, f32[4,4,8,1536]{3,2,1,0:T(8,128)}, f32[4,4,8,1536]{3,2,1,0:T(8,128)}, f32[1,128]{1,0:T(1,128)}) custom-call(s32[1,128]{1,0:T(1,128)} %bitcast.9, s32[1,128]{1,0:T(1,128)} %bitcast.10, s32[1,128]{1,0:T(1,128)} %bitcast.11, f32[16,8,1536]{2,1,0:T(8,128)} %refs_0_.1, f32[16,8,1536]{2,1,0:T(8,128)} %refs_1_.1, ...), custom_call_target="tpu_custom_call" | custom-call | tf_op jit(solution)/shard_map/exchange/pallas_call | solution.py:273
  63.5 4.4 %adam.1 = (f32[1,128,1536]{2,1,0:T(8,128)}, f32[1,128,1536]{2,1,0:T(8,128)}, f32[1,128,1536]{2,1,0:T(8,128)}) custom-call(f32[1,128]{1,0:T(1,128)} %get-tuple-element.7.slot_count, f32[1,128,1536]{2,1,0:T(8,128)} %bitcast.6, f32[1,128,1536]{2,1,0:T(8,128)} %bitcast.7, f32[1,128,1536]{2,1,0:T(8,128)} %bitcast.8, bf16[1,128,1536]{2,1,0:T(8,128)(2,1)} %grad.1), custom_call_target="tpu_custom_call" | custom-call | tf_op jit(solution)/shard_map/adam/pallas_call | solution.py:240

commit v3 on v2

--- a/solution.py
+++ b/solution.py
@@ -13,6 +13,9 @@
 Z_LAG = 2
 Y_LAG = 4
 ADAM_ROWS = 32
+DEPTH = 2
+TIERS = ((9, 9), (10, 10))
+WIDTHS = ((2, 2, 2), (2, 2, 2), (2, 2, 1, 1))
 
 first_correction = 1.0 - 0.9**10
 second_correction = 1.0 - 0.999**10
@@ -27,7 +30,7 @@
 
 
 def exchange_kernel(
-    chunks, quarter, counts_ref, old_owner_ref, new_owner_ref, *refs
+    chunks, quarter, table_ref, counts_ref, old_owner_ref, new_owner_ref, *refs
 ):
     states, (outs, slot_count_ref), scratch = refs[:3], (refs[3:6], refs[6]), refs[7:]
     n = len(chunks)
@@ -223,6 +226,305 @@
     return device(x, y, z, other)
 
 
+def plan_kernel(old_owner_ref, new_owner_ref, table_ref):
+    f32, i32 = jnp.float32, jnp.int32
+    square, row = (LANES, LANES), (8, LANES)
+    old, new = (jnp.broadcast_to(ref[...], square) for ref in (old_owner_ref, new_owner_ref))
+    sub, lane = lax.broadcasted_iota(i32, square, 0), lax.broadcasted_iota(i32, square, 1)
+
+    dest_down = jnp.sum(jnp.where(old == sub, new, 0).astype(f32), axis=1, keepdims=True)
+    dest_down = jnp.broadcast_to(dest_down, square)
+    dest_across = dest_down.T.astype(i32)
+    dest_down = dest_down.astype(i32)
+    shift_down = ((dest_down >> 5) - (sub >> 5)) & 3
+    shift_across = ((dest_across >> 5) - (lane >> 5)) & 3
+    together = (sub >> 5) == (lane >> 5)
+
+    def tally(mask):
+        return jnp.broadcast_to(jnp.sum(jnp.where(mask, 1, 0), axis=0, keepdims=True), row)
+
+    rank = tally(together & (shift_down == shift_across) & (sub < lane))
+    n1, n2, n3 = (tally(together & (shift_down == d)) for d in (1, 2, 3))
+
+    lane = lane[:8]
+    slot, shift, home, own = dest_across[:8], shift_across[:8], lane >> 5, lane & 31
+
+    def before(v):
+        return pltpu.roll(v, 32, 1)
+
+    def after(v):
+        return pltpu.roll(v, LANES - 32, 1)
+
+    def loads(up):
+        down = n2 - up
+        return n1 + up + before(up), n3 + down + after(down)
+
+    up = (n2 + (home & 1)) >> 1
+    for parity in (0, 1):
+        plus, minus = loads(up)
+        gap = jnp.maximum(minus, before(minus)) - jnp.maximum(plus, after(plus))
+        step = jnp.where(gap < 0, -((-gap) >> 1), gap >> 1)
+        up = jnp.where((home & 1) == parity, jnp.clip(up + step, 0, n2), up)
+    down = n2 - up
+    plus, minus = loads(up)
+
+    def highest(v):
+        return jnp.broadcast_to(jnp.max(v.astype(f32), axis=1, keepdims=True), row).astype(i32)
+
+    need, need_far = highest(jnp.maximum(plus, minus)), highest(jnp.maximum(up, down))
+    tier = jnp.full(row, len(TIERS), i32)
+    first, second = jnp.full(row, TIERS[-1][0], i32), jnp.full(row, TIERS[-1][1], i32)
+    for number, (l1, l2) in reversed(list(enumerate(TIERS))):
+        fits = (need <= l1 + l2) & (need_far <= min(l1, l2))
+        tier = jnp.where(fits, number, tier)
+        first, second = jnp.where(fits, l1, first), jnp.where(fits, l2, second)
+
+    here = lax.div(lax.axis_index("gx"), 2)
+    mine, from_before, from_after = (
+        home == here,
+        home == lax.rem(here + 3, 4),
+        home == lax.rem(here + 1, 4),
+    )
+    goes_up = rank < up
+    at_up, at_down = up + rank, down + rank
+    late_up, late_down = before(up) + at_up - first, after(down) + at_down - first
+    one, two, three = shift == 1, shift == 2, shift == 3
+
+    def pick(*cases):
+        value = jnp.full(row, -1, i32)
+        for mask, case in cases:
+            value = jnp.where(mask, case, value)
+        return value
+
+    sends = (
+        (pick((mine & two & goes_up, rank), (mine & one & (at_up < first), at_up)), own),
+        (pick((mine & two & ~goes_up, rank - up), (mine & three & (at_down < first), at_down)), own),
+        (
+            pick((mine & one & (at_up >= first), late_up), (from_before & two & goes_up, rank)),
+            pick((mine, own), (from_before, 32 + rank)),
+        ),
+        (
+            pick((mine & three & (at_down >= first), late_down), (from_after & two & ~goes_up, rank - up)),
+            pick((mine, own), (from_after, 32 + first + rank - up)),
+        ),
+        (
+            pick(((slot >> 5) == here, slot & 31)),
+            pick(
+                (shift == 0, own),
+                (one & (at_up < first), 32 + at_up),
+                (one & (at_up >= first), 32 + 2 * first + late_up),
+                (three & (at_down < first), 32 + first + at_down),
+                (three & (at_down >= first), 32 + 2 * first + second + late_down),
+                (two & goes_up, 32 + 2 * first + rank),
+                (two & ~goes_up, 32 + 2 * first + second + rank - up),
+            ),
+        ),
+    )
+    places = lax.broadcasted_iota(i32, (32, LANES), 0)
+    lanes = lax.broadcasted_iota(i32, (32, LANES), 1)
+    table = jnp.where(lanes == 5, tier[:1], 0).astype(f32)
+    for k, (position, value) in enumerate(sends):
+        hit = jnp.broadcast_to(position[:1], (32, LANES)) == places
+        entry = jnp.sum(jnp.where(hit, value[:1], 0).astype(f32), axis=1, keepdims=True)
+        table = jnp.where(lanes == k, entry, table)
+    table = jnp.concatenate([table, jnp.zeros((LANES - 32, LANES), f32)], axis=0)
+    table_ref[...] = table.T[:8].astype(i32)
+
+
+def routed_kernel(chunks, half, l1, l2, table_ref, counts_ref, old_owner_ref, new_owner_ref, *refs):
+    states, (outs, slot_count_ref), scratch = refs[:3], (refs[3:6], refs[6]), refs[7:]
+    n = len(chunks)
+    pools, landed, b1, b2, b3, held = (scratch[i * n : (i + 1) * n] for i in range(6))
+    count_g, count_x, count_z, sx, sz, owners, plan = scratch[6 * n : 6 * n + 7]
+    own_sem, core_send, core_recv, r_send, r_recv, x_send, x_recv = scratch[6 * n + 7 : 6 * n + 14]
+    z_send, z_recv, out_sem, n_send, n_recv, small_sem = scratch[6 * n + 14 :]
+
+    gx, gy = lax.axis_index("gx"), lax.axis_index("gy")
+    x, y, z, c = lax.div(gy, 4), lax.div(gx, 2), lax.rem(gy, 4), lax.rem(gx, 2)
+    other = 1 - c
+    xs = [device(mod4(x + d), y, z, c) for d in range(4)]
+    zs = [device(x, y, mod4(z + d), c) for d in range(4)]
+    zo = [device(x, y, mod4(z + d), other) for d in range(4)]
+    gs = [(lax.rem(gx + d, 8), gy) for d in range(8)]
+    above, below = device(x, mod4(y + 1), z, c), device(x, mod4(y - 1), z, c)
+
+    barrier = pltpu.get_barrier_semaphore()
+    for peer in gs[1:] + xs[1:] + zs[1:] + zo[1:]:
+        pl.semaphore_signal(barrier, inc=1, device_id=peer, device_id_type=MESH)
+    small = [
+        pltpu.make_async_copy(table_ref, plan, small_sem.at[0]),
+        pltpu.make_async_copy(new_owner_ref, owners.at[0], small_sem.at[1]),
+        pltpu.make_async_copy(counts_ref, count_g.at[gx], small_sem.at[2]),
+    ]
+    for copy in small:
+        copy.start()
+
+    def columns(owner_c, offset, width):
+        return pl.ds(pl.multiple_of(owner_c * half + offset, LANES), width)
+
+    sixteen = pl.ds(pl.multiple_of(c * 16, 16), 16)
+    own = []
+    for k, (s, offset, width) in enumerate(chunks):
+        own.append(
+            pltpu.make_async_copy(
+                states[s].at[:, :, columns(c, offset, width)], pools[k].at[sixteen], own_sem.at[k]
+            )
+        )
+        own[k].start()
+    pl.semaphore_wait(barrier, 16)
+
+    started = []
+
+    def remote(src, dst, send, recv, peer):
+        copy = pltpu.make_async_remote_copy(
+            src_ref=src, dst_ref=dst, send_sem=send, recv_sem=recv, device_id=peer, device_id_type=MESH
+        )
+        copy.start()
+        started.append(copy)
+        return copy
+
+    swapped = [
+        remote(
+            states[s].at[:, :, columns(other, offset, width)],
+            pools[k].at[sixteen],
+            core_send.at[k],
+            core_recv.at[k],
+            zo[0],
+        )
+        for k, (s, offset, width) in enumerate(chunks)
+    ]
+    for copy in small:
+        copy.wait()
+    counted = [remote(counts_ref, count_g.at[gx], n_send.at[d], n_recv.at[d], gs[d]) for d in range(1, 8)]
+
+    def tally_x(copies):
+        for copy in copies:
+            copy.wait_recv()
+        count = jnp.sum(count_g[...].astype(jnp.float32), axis=0)
+        sx[...] = count
+        count_x[pl.ds(x, 1)] = count.reshape(1, 1, LANES)
+
+    def tally_send_x():
+        return [remote(sx, count_x.at[x], n_send.at[7 + d], n_recv.at[7 + d], xs[d]) for d in range(1, 4)]
+
+    def tally_z(copies):
+        for copy in copies:
+            copy.wait_recv()
+        count = jnp.sum(count_x[...], axis=0)
+        sz[...] = count
+        count_z[pl.ds(z, 1)] = count.reshape(1, 1, LANES)
+
+    def tally_send_z():
+        return [remote(sz, count_z.at[z], n_send.at[10 + d], n_recv.at[10 + d], zs[d]) for d in range(1, 4)]
+
+    round1, round2, sent_x, sent_z = {}, {}, {}, {}
+
+    def pick(k, entry, arrived):
+        here = pools[k][jnp.minimum(entry, 31)]
+        return jnp.where(jnp.full(here.shape, entry, jnp.int32) < 32, here, arrived)
+
+    def steps(size, place):
+        lax.fori_loop(0, size, place, 0, unroll=size if size % 2 else size // 2)
+
+    def first_round(k):
+        own[k].wait()
+        swapped[k].wait_recv()
+
+        def place(j, carry):
+            for side in range(2):
+                b1[k][side, j] = pools[k][plan[side, j]]
+            return carry
+
+        steps(l1, place)
+        round1[k] = [
+            remote(b1[k].at[0], landed[k].at[pl.ds(0, l1)], r_send.at[k, 0], r_recv.at[k, 0], above),
+            remote(b1[k].at[1], landed[k].at[pl.ds(l1, l1)], r_send.at[k, 1], r_recv.at[k, 1], below),
+        ]
+
+    def second_round(k):
+        for copy in round1[k]:
+            copy.wait_recv()
+
+        def place(j, carry):
+            for side in range(2):
+                b2[k][side, j] = pick(k, plan[2 + side, j], landed[k][side * l1 + j])
+            return carry
+
+        steps(l2, place)
+        base = 2 * l1
+        round2[k] = [
+            remote(b2[k].at[0], landed[k].at[pl.ds(base, l2)], r_send.at[k, 2], r_recv.at[k, 2], above),
+            remote(b2[k].at[1], landed[k].at[pl.ds(base + l2, l2)], r_send.at[k, 3], r_recv.at[k, 3], below),
+        ]
+
+    def along_x(k):
+        for copy in round2[k]:
+            copy.wait_recv()
+        for d in ORDER + (0,):
+            base = 4 * mod4(x + d)
+
+            def place(j, carry, d=d, base=base):
+                to_z, to_c = lax.div(j, 2), lax.rem(j, 2)
+                entry = plan[4, base + 16 * to_c + to_z]
+                tile = pick(k, entry, landed[k][jnp.maximum(entry - 32, 0)])
+                if d == 0:
+                    held[k][x, to_z, to_c] = tile
+                else:
+                    b3[k][d - 1, to_z, to_c] = tile
+                return carry
+
+            lax.fori_loop(0, 8, place, 0, unroll=8)
+        sent_x[k] = [remote(b3[k].at[d - 1], held[k].at[x], x_send.at[k, d], x_recv.at[k, d], xs[d]) for d in ORDER]
+
+    def along_z(k):
+        s, offset, width = chunks[k]
+        for copy in sent_x[k]:
+            copy.wait_recv()
+        landing = outs[s].at[:, z, :, columns(c, offset, width)]
+        sent_z[k] = []
+        for d in ORDER + (0,):
+            to_z = mod4(z + d)
+            sent_z[k].append(
+                remote(held[k].at[:, to_z, other], landing, z_send.at[k, 4 + d], z_recv.at[k, 4 + d], zo[d])
+            )
+            if d:
+                sent_z[k].append(remote(held[k].at[:, to_z, c], landing, z_send.at[k, d], z_recv.at[k, d], zs[d]))
+        local = pltpu.make_async_copy(held[k].at[:, z, c], landing, out_sem.at[k])
+        local.start()
+        own[k] = local
+
+    for k in range(min(DEPTH, n)):
+        first_round(k)
+    for i in range(n + 3):
+        if i < n:
+            second_round(i)
+        if i + DEPTH < n:
+            first_round(i + DEPTH)
+        if 0 <= i - 3 < n:
+            along_z(i - 3)
+        if 0 <= i - 1 < n:
+            along_x(i - 1)
+        if i == 0:
+            tally_x(counted)
+        if i == 1:
+            counted = tally_send_x()
+        if i == 3:
+            tally_z(counted)
+        if i == 4:
+            counted = tally_send_z()
+    for copy in counted:
+        copy.wait_recv()
+    totals = jnp.sum(count_z[...], axis=0)
+    mine = jnp.where(owners[0] == gx * 16 + gy, totals, 0.0)
+    slot_count_ref[...] = jnp.broadcast_to(jnp.sum(mine, axis=1, keepdims=True), (1, LANES))
+    for k in range(n):
+        own[k].wait()
+        for copy in sent_z[k]:
+            copy.wait_recv()
+    for copy in started:
+        copy.wait_send()
+
+
 def adam_kernel(slot_count, master, first, second, grad, new_master, new_first, new_second):
     scaled = grad[0].astype(jnp.float32) / slot_count[0:1, 0:1]
     moved_first = 0.9 * first[0] + 0.1 * scaled
@@ -249,38 +551,94 @@
 
 def body(old_master, old_first, old_second, new_grad, counts, old_owner, new_owner):
     experts = old_owner.shape[0]
-    group, rows, ff = old_master.shape
-    quarter = ff // 4
+    _, rows, ff = old_master.shape
+    quarter, half = ff // 4, ff // 2
     row = (1, experts)
+    f32, i32 = jnp.float32, jnp.int32
+    dma = pltpu.SemaphoreType.DMA
+    landed = jax.ShapeDtypeStruct((4, 4, rows, ff), f32)
+    vmem, hbm = pl.BlockSpec(memory_space=pltpu.VMEM), pl.BlockSpec(memory_space=pl.ANY)
+
+    def exchange(kernel, name, number, scratch):
+        def run(*operands):
+            return pl.pallas_call(
+                kernel,
+                name=name,
+                out_shape=(landed, landed, landed, jax.ShapeDtypeStruct(row, f32)),
+                in_specs=[hbm] * 7,
+                out_specs=(hbm, hbm, hbm, vmem),
+                scratch_shapes=scratch,
+                compiler_params=pltpu.CompilerParams(
+                    collective_id=number, has_side_effects=True, vmem_limit_bytes=60 * 1024 * 1024
+                ),
+            )(*operands)
+
+        return run
+
+    tallies = [pltpu.VMEM((8, 1, experts), i32), pltpu.VMEM((4, 1, experts), f32), pltpu.VMEM((4, 1, experts), f32)]
+    tallies += [pltpu.VMEM(row, f32), pltpu.VMEM(row, f32)]
 
     chunks = [(s, offset, LANES) for s in range(3) for offset in range(0, quarter, LANES)]
     n = len(chunks)
-    f32 = jnp.float32
-    dma = pltpu.SemaphoreType.DMA
-    scratch = (
+    spread = exchange(
+        functools.partial(exchange_kernel, chunks, quarter),
+        "spread",
+        len(TIERS),
         [pltpu.VMEM((experts, rows, w), f32) for _, _, w in chunks]
         + [pltpu.VMEM((3, 4, 4, rows, w), f32) for _, _, w in chunks]
         + [pltpu.VMEM((4, 4, 4, rows, w), f32) for _, _, w in chunks]
         + [pltpu.VMEM((4, 4, 4, rows, w), f32) for _, _, w in chunks]
-        + [pltpu.VMEM((8, 1, experts), jnp.int32), pltpu.VMEM((4, 1, experts), f32), pltpu.VMEM((4, 1, experts), f32)]
-        + [pltpu.VMEM((1, experts), f32), pltpu.VMEM((1, experts), f32), pltpu.VMEM((2, 1, experts), jnp.int32)]
-        + [pltpu.VMEM((1, experts), jnp.int32), pltpu.SMEM((1, experts), jnp.int32)]
+        + tallies
+        + [pltpu.VMEM((2, 1, experts), i32), pltpu.VMEM(row, i32), pltpu.SMEM(row, i32)]
         + [dma((n, 4)), dma((n, 4)), dma((n,)), dma((n, 4)), dma((n, 4)), dma((n, 4)), dma((n, 4))]
-        + [dma((n, 4)), dma((n, 4)), dma((n, 4)), dma((n, 4)), dma((n,)), dma((14,)), dma((14,)), dma((4,))]
+        + [dma((n, 4)), dma((n, 4)), dma((n, 4)), dma((n, 4)), dma((n,)), dma((14,)), dma((14,)), dma((4,))],
     )
-    landed = jax.ShapeDtypeStruct((4, 4, rows, ff), f32)
-    vmem, hbm = pl.BlockSpec(memory_space=pltpu.VMEM), pl.BlockSpec(memory_space=pl.ANY)
-    master, first, second, slot_count = pl.pallas_call(
-        functools.partial(exchange_kernel, chunks, quarter),
-        name="exchange",
-        out_shape=(landed, landed, landed, jax.ShapeDtypeStruct((1, experts), f32)),
-        in_specs=[hbm] * 6,
-        out_specs=(hbm, hbm, hbm, vmem),
-        scratch_shapes=scratch,
-        compiler_params=pltpu.CompilerParams(
-            collective_id=0, has_side_effects=True, vmem_limit_bytes=60 * 1024 * 1024
-        ),
-    )(counts.reshape(row), old_owner.reshape(row), new_owner.reshape(row), old_master, old_first, old_second)
+
+    pieces = []
+    for s, widths in enumerate(WIDTHS):
+        offset = 0
+        for tiles in widths:
+            pieces.append((s, offset, tiles * LANES))
+            offset += tiles * LANES
+    m = len(pieces)
+    branches = [
+        exchange(
+            functools.partial(routed_kernel, pieces, half, l1, l2),
+            f"routed_{l1 + l2}",
+            number,
+            [pltpu.VMEM((32, rows, w), f32) for _, _, w in pieces]
+            + [pltpu.VMEM((2 * l1 + 2 * l2, rows, w), f32) for _, _, w in pieces]
+            + [pltpu.VMEM((2, l1, rows, w), f32) for _, _, w in pieces]
+            + [pltpu.VMEM((2, l2, rows, w), f32) for _, _, w in pieces]
+            + [pltpu.VMEM((3, 4, 2, rows, w), f32) for _, _, w in pieces]
+            + [pltpu.VMEM((4, 4, 2, rows, w), f32) for _, _, w in pieces]
+            + tallies
+            + [pltpu.VMEM((1, 1, experts), i32), pltpu.SMEM((8, experts), i32)]
+            + [dma((m,)), dma((m,)), dma((m,)), dma((m, 4)), dma((m, 4)), dma((m, 4)), dma((m, 4))]
+            + [dma((m, 8)), dma((m, 8)), dma((m,)), dma((14,)), dma((14,)), dma((3,))],
+        )
+        for number, (l1, l2) in enumerate(TIERS)
+    ]
+
+    old, new = old_owner.reshape(row), new_owner.reshape(row)
+    table = pl.pallas_call(
+        plan_kernel,
+        name="plan",
+        out_shape=jax.ShapeDtypeStruct((8, experts), i32),
+        in_specs=[vmem, vmem],
+        out_specs=vmem,
+    )(old, new)
+    master, first, second, slot_count = lax.switch(
+        table[5, 0],
+        branches + [spread],
+        table,
+        counts.reshape(row),
+        old,
+        new,
+        old_master,
+        old_first,
+        old_second,
+    )
     shape = (1, 16 * rows, ff)
     return adam_step(master.reshape(shape), first.reshape(shape), second.reshape(shape), new_grad, slot_count)
 

time: 68.5 us -> 65 us (0.949)
  Pallas kernels: 67.2 us -> 61.4 us
  local copies, waits for them, and re-layouts: 0 us -> 1.83 us
    pallas_call x1 -> x2, Pallas kernels: 62.9 us -> 57.6 us  [the longest x1 56.8 us: run(): pl.pallas_call(kernel, name=name, out_shape=(landed, landed, landed, jax....]
    unnamed x0 -> x6, local copies, waits for them, and re-layouts: none -> 1.31 us
where the time goes in v3:
time: 65 us; the launch traced here: 64.8 us
  Pallas kernels  61.4 us (94%)
  local copies, waits for them, and re-layouts  1.83 us (3%)
  between operations  1.32 us (2%)
    pallas_call x1, Pallas kernels, run(): pl.pallas_call(kernel, name=name, out_shape=(landed, landed, landed, jax....  56.8 us
    pallas_call x1, Pallas kernels, adam_step(): pl.pallas_call(adam_kernel, name='adam', grid=(rows // block_rows,), out_...  3.81 us
    unnamed x6, local copies, waits for them, and re-layouts  1.31 us

profile of v3, /device:TPU:1, one launch (start us, length us, event | category | flops | bytes accessed | tf_op | source)
XLA Modules:
  0.0 64.8 jit_solution(4976895332086070662)
XLA Ops:
  0.6 0.0 copy-start
  0.6 0.0 copy-start.1
  0.7 0.6 copy-done
  1.3 0.0 copy-done.1
  1.3 0.7 %plan.1 = s32[8,128]{1,0:T(8,128)S(1)} custom-call(s32[1,128]{1,0:T(1,128)S(1)} %bitcast.10, s32[1,128]{1,0:T(1,128)S(1)} %bitcast.14), custom_call_target="tpu_custom_call" | custom-call | tf_op jit(solution)/shard_map/plan/pallas_call | solution.py:624
  2.0 0.5 slice.3
  3.2 0.0 copy-start.2
  3.2 0.6 copy-done.2
  3.9 57.1 %conditional.1 = ((f32[4,4,8,1536]{3,2,1,0:T(8,128)S(1)}, f32[4,4,8,1536]{3,2,1,0:T(8,128)S(1)}, f32[4,4,8,1536]{3,2,1,0:T(8,128)S(1)}, f32[1,128]{1,0:T(1,128)S(1)})) conditional(s32[]{:T(128)} %bitcast.2, (s32[8,128]{1,0:T(8,128)S(1)}, s32[1,128]{1,0:T(1,128)S(1)}, s32[1,128]{1,0:T(1,128)S(1)}, s32[1,128]{1,0:T(1,128)S(1)}, ...), branch_computations={%region_0.0_spmd, %region_1.0_spmd, %region_2.0_spmd} | conditional | bytes 8 | solution.py:631
  3.9 56.8 %routed_18.1 = (f32[4,4,8,1536]{3,2,1,0:T(8,128)S(1)}, f32[4,4,8,1536]{3,2,1,0:T(8,128)S(1)}, f32[4,4,8,1536]{3,2,1,0:T(8,128)S(1)}, f32[1,128]{1,0:T(1,128)S(1)}) custom-call(s32[8,128]{1,0:T(8,128)S(1)} %get-tuple-element.62.table_ref, s32[1,128]{1,0:T(1,128)S(1)} %get-tuple-element.63.counts_ref, s32[1,128]{1,0:T(1,128)S(1)} %get-tuple-element.64.old_owner_ref, ...), custom_call_target="tpu_custom_call" | custom-call | tf_op jit(solution)/shard_map/cond/branch_0_fun/routed_18/pallas_call | solution.py:564
  61.0 3.8 %adam.1 = (f32[1,128,1536]{2,1,0:T(8,128)}, f32[1,128,1536]{2,1,0:T(8,128)}, f32[1,128,1536]{2,1,0:T(8,128)}) custom-call(f32[1,128]{1,0:T(1,128)S(1)} %get-tuple-element.113.slot_count, f32[1,128,1536]{2,1,0:T(8,128)S(1)} %bitcast.7, f32[1,128,1536]{2,1,0:T(8,128)S(1)} %bitcast.8, f32[1,128,1536]{2,1,0:T(8,128)S(1)} %bitcast.9, bf16[1,128,1536]{2,1,0:T(8,128)(2,1)} %grad.1), custom_call_target="tpu_custom_call" | custom-call | tf_op jit(solution)/shard_map/adam/pallas_call | solution.py:542
Async XLA Ops:
  0.6 0.7 %copy-start = (s32[128]{0:T(128)S(1)}, s32[128]{0:T(128)}, u32[]{:S(2)}) copy-start(s32[128]{0:T(128)} %param.15) | copy-start | bytes 1540
  0.6 0.7 %copy-start.1 = (s32[128]{0:T(128)S(1)}, s32[128]{0:T(128)}, u32[]{:S(2)}) copy-start(s32[128]{0:T(128)} %param.16) | copy-start | bytes 1540
  3.2 0.7 %copy-start.2 = (s32[128,1]{0,1:T(1,128)S(1)}, s32[128,1]{0,1:T(1,128)}, u32[]{:S(2)}) copy-start(s32[128,1]{0,1:T(1,128)} %param.14) | copy-start | bytes 1540

commit v4 on v3

--- a/solution.py
+++ b/solution.py
@@ -12,10 +12,13 @@
 ORDER = (1, 3, 2)
 Z_LAG = 2
 Y_LAG = 4
-ADAM_ROWS = 32
-DEPTH = 2
-TIERS = ((9, 9), (10, 10))
-WIDTHS = ((2, 2, 2), (2, 2, 2), (2, 2, 1, 1))
+ADAM_ROWS = 16
+DEPTH = 4
+X_AFTER = 3
+Z_AFTER = 7
+TALLY = 2
+TIERS = ((8, 8), (9, 8), (9, 9), (10, 10))
+WIDTHS = ((1,) * 6,) * 3
 
 first_correction = 1.0 - 0.9**10
 second_correction = 1.0 - 0.999**10
@@ -226,7 +229,8 @@
     return device(x, y, z, other)
 
 
-def plan_kernel(old_owner_ref, new_owner_ref, table_ref):
+def plan_kernel(old_owner_ref, new_owner_ref, counts_ref, table_ref, tally_ref, tier_ref):
+    tally_ref[...] = counts_ref[...]
     f32, i32 = jnp.float32, jnp.int32
     square, row = (LANES, LANES), (8, LANES)
     old, new = (jnp.broadcast_to(ref[...], square) for ref in (old_owner_ref, new_owner_ref))
@@ -322,7 +326,8 @@
     )
     places = lax.broadcasted_iota(i32, (32, LANES), 0)
     lanes = lax.broadcasted_iota(i32, (32, LANES), 1)
-    table = jnp.where(lanes == 5, tier[:1], 0).astype(f32)
+    tier_ref[0] = jnp.max(tier.astype(f32)).astype(i32)
+    table = jnp.zeros((32, LANES), f32)
     for k, (position, value) in enumerate(sends):
         hit = jnp.broadcast_to(position[:1], (32, LANES)) == places
         entry = jnp.sum(jnp.where(hit, value[:1], 0).astype(f32), axis=1, keepdims=True)
@@ -336,8 +341,7 @@
     n = len(chunks)
     pools, landed, b1, b2, b3, held = (scratch[i * n : (i + 1) * n] for i in range(6))
     count_g, count_x, count_z, sx, sz, owners, plan = scratch[6 * n : 6 * n + 7]
-    own_sem, core_send, core_recv, r_send, r_recv, x_send, x_recv = scratch[6 * n + 7 : 6 * n + 14]
-    z_send, z_recv, out_sem, n_send, n_recv, small_sem = scratch[6 * n + 14 :]
+    meter, own_sem, send, arrive, n_send, n_recv, small_sem = scratch[6 * n + 7 :]
 
     gx, gy = lax.axis_index("gx"), lax.axis_index("gy")
     x, y, z, c = lax.div(gy, 4), lax.div(gx, 2), lax.rem(gy, 4), lax.rem(gx, 2)
@@ -373,51 +377,42 @@
         own[k].start()
     pl.semaphore_wait(barrier, 16)
 
-    started = []
-
-    def remote(src, dst, send, recv, peer):
-        copy = pltpu.make_async_remote_copy(
-            src_ref=src, dst_ref=dst, send_sem=send, recv_sem=recv, device_id=peer, device_id_type=MESH
+    def remote(src, dst, sent, landing, peer):
+        pltpu.make_async_remote_copy(
+            src_ref=src, dst_ref=dst, send_sem=sent, recv_sem=landing, device_id=peer, device_id_type=MESH
+        ).start()
+
+    def settle(sem, ref):
+        pltpu.make_async_copy(ref, ref, sem).wait()
+
+    for k, (s, offset, width) in enumerate(chunks):
+        remote(
+            states[s].at[:, :, columns(other, offset, width)], pools[k].at[sixteen], send.at[k], arrive.at[k, 0], zo[0]
         )
-        copy.start()
-        started.append(copy)
-        return copy
-
-    swapped = [
-        remote(
-            states[s].at[:, :, columns(other, offset, width)],
-            pools[k].at[sixteen],
-            core_send.at[k],
-            core_recv.at[k],
-            zo[0],
-        )
-        for k, (s, offset, width) in enumerate(chunks)
-    ]
     for copy in small:
         copy.wait()
-    counted = [remote(counts_ref, count_g.at[gx], n_send.at[d], n_recv.at[d], gs[d]) for d in range(1, 8)]
-
-    def tally_x(copies):
-        for copy in copies:
-            copy.wait_recv()
+    for peer in gs[1:]:
+        remote(counts_ref, count_g.at[gx], n_send.at[0], n_recv.at[0], peer)
+
+    def tally_x():
+        settle(n_recv.at[0], count_g.at[pl.ds(0, 7)])
         count = jnp.sum(count_g[...].astype(jnp.float32), axis=0)
         sx[...] = count
         count_x[pl.ds(x, 1)] = count.reshape(1, 1, LANES)
 
     def tally_send_x():
-        return [remote(sx, count_x.at[x], n_send.at[7 + d], n_recv.at[7 + d], xs[d]) for d in range(1, 4)]
-
-    def tally_z(copies):
-        for copy in copies:
-            copy.wait_recv()
+        for peer in xs[1:]:
+            remote(sx, count_x.at[x], n_send.at[1], n_recv.at[1], peer)
+
+    def tally_z():
+        settle(n_recv.at[1], count_x.at[pl.ds(0, 3)])
         count = jnp.sum(count_x[...], axis=0)
         sz[...] = count
         count_z[pl.ds(z, 1)] = count.reshape(1, 1, LANES)
 
     def tally_send_z():
-        return [remote(sz, count_z.at[z], n_send.at[10 + d], n_recv.at[10 + d], zs[d]) for d in range(1, 4)]
-
-    round1, round2, sent_x, sent_z = {}, {}, {}, {}
+        for peer in zs[1:]:
+            remote(sz, count_z.at[z], n_send.at[2], n_recv.at[2], peer)
 
     def pick(k, entry, arrived):
         here = pools[k][jnp.minimum(entry, 31)]
@@ -428,7 +423,7 @@
 
     def first_round(k):
         own[k].wait()
-        swapped[k].wait_recv()
+        settle(arrive.at[k, 0], pools[k].at[pl.ds(0, 16)])
 
         def place(j, carry):
             for side in range(2):
@@ -436,14 +431,11 @@
             return carry
 
         steps(l1, place)
-        round1[k] = [
-            remote(b1[k].at[0], landed[k].at[pl.ds(0, l1)], r_send.at[k, 0], r_recv.at[k, 0], above),
-            remote(b1[k].at[1], landed[k].at[pl.ds(l1, l1)], r_send.at[k, 1], r_recv.at[k, 1], below),
-        ]
+        remote(b1[k].at[0], landed[k].at[pl.ds(0, l1)], send.at[k], arrive.at[k, 1], above)
+        remote(b1[k].at[1], landed[k].at[pl.ds(l1, l1)], send.at[k], arrive.at[k, 1], below)
 
     def second_round(k):
-        for copy in round1[k]:
-            copy.wait_recv()
+        settle(arrive.at[k, 1], landed[k].at[pl.ds(0, 2 * l1)])
 
         def place(j, carry):
             for side in range(2):
@@ -452,14 +444,11 @@
 
         steps(l2, place)
         base = 2 * l1
-        round2[k] = [
-            remote(b2[k].at[0], landed[k].at[pl.ds(base, l2)], r_send.at[k, 2], r_recv.at[k, 2], above),
-            remote(b2[k].at[1], landed[k].at[pl.ds(base + l2, l2)], r_send.at[k, 3], r_recv.at[k, 3], below),
-        ]
+        remote(b2[k].at[0], landed[k].at[pl.ds(base, l2)], send.at[k], arrive.at[k, 2], above)
+        remote(b2[k].at[1], landed[k].at[pl.ds(base + l2, l2)], send.at[k], arrive.at[k, 2], below)
 
     def along_x(k):
-        for copy in round2[k]:
-            copy.wait_recv()
+        settle(arrive.at[k, 2], landed[k].at[pl.ds(2 * l1, 2 * l2)])
         for d in ORDER + (0,):
             base = 4 * mod4(x + d)
 
@@ -474,78 +463,98 @@
                 return carry
 
             lax.fori_loop(0, 8, place, 0, unroll=8)
-        sent_x[k] = [remote(b3[k].at[d - 1], held[k].at[x], x_send.at[k, d], x_recv.at[k, d], xs[d]) for d in ORDER]
+        for d in ORDER:
+            remote(b3[k].at[d - 1], held[k].at[x], send.at[k], arrive.at[k, 3], xs[d])
 
     def along_z(k):
         s, offset, width = chunks[k]
-        for copy in sent_x[k]:
-            copy.wait_recv()
+        settle(arrive.at[k, 3], held[k].at[pl.ds(0, 3)])
         landing = outs[s].at[:, z, :, columns(c, offset, width)]
-        sent_z[k] = []
         for d in ORDER + (0,):
             to_z = mod4(z + d)
-            sent_z[k].append(
-                remote(held[k].at[:, to_z, other], landing, z_send.at[k, 4 + d], z_recv.at[k, 4 + d], zo[d])
-            )
+            remote(held[k].at[:, to_z, other], landing, send.at[k], arrive.at[k, 4], zo[d])
             if d:
-                sent_z[k].append(remote(held[k].at[:, to_z, c], landing, z_send.at[k, d], z_recv.at[k, d], zs[d]))
-        local = pltpu.make_async_copy(held[k].at[:, z, c], landing, out_sem.at[k])
+                remote(held[k].at[:, to_z, c], landing, send.at[k], arrive.at[k, 4], zs[d])
+        local = pltpu.make_async_copy(held[k].at[:, z, c], landing, own_sem.at[k])
         local.start()
         own[k] = local
 
     for k in range(min(DEPTH, n)):
         first_round(k)
-    for i in range(n + 3):
+    for i in range(n + Z_AFTER):
         if i < n:
             second_round(i)
         if i + DEPTH < n:
             first_round(i + DEPTH)
-        if 0 <= i - 3 < n:
-            along_z(i - 3)
-        if 0 <= i - 1 < n:
-            along_x(i - 1)
-        if i == 0:
-            tally_x(counted)
-        if i == 1:
-            counted = tally_send_x()
-        if i == 3:
-            tally_z(counted)
-        if i == 4:
-            counted = tally_send_z()
-    for copy in counted:
-        copy.wait_recv()
+        if 0 <= i - Z_AFTER < n:
+            along_z(i - Z_AFTER)
+        if 0 <= i - X_AFTER < n:
+            along_x(i - X_AFTER)
+        if i == TALLY:
+            tally_x()
+        if i == TALLY + 1:
+            tally_send_x()
+        if i == TALLY + 3:
+            tally_z()
+        if i == TALLY + 4:
+            tally_send_z()
+    settle(n_recv.at[2], count_z.at[pl.ds(0, 3)])
     totals = jnp.sum(count_z[...], axis=0)
     mine = jnp.where(owners[0] == gx * 16 + gy, totals, 0.0)
     slot_count_ref[...] = jnp.broadcast_to(jnp.sum(mine, axis=1, keepdims=True), (1, LANES))
-    for k in range(n):
+    for k, (_, _, width) in enumerate(chunks):
         own[k].wait()
-        for copy in sent_z[k]:
-            copy.wait_recv()
-    for copy in started:
-        copy.wait_send()
-
-
-def adam_kernel(slot_count, master, first, second, grad, new_master, new_first, new_second):
-    scaled = grad[0].astype(jnp.float32) / slot_count[0:1, 0:1]
-    moved_first = 0.9 * first[0] + 0.1 * scaled
-    moved_second = 0.999 * second[0] + 0.001 * scaled * scaled
-    step_dir = moved_first / first_correction / (jnp.sqrt(moved_second / second_correction) + 1e-08)
-    new_master[0] = master[0] - 0.01 * (step_dir + 0.1 * master[0])
-    new_first[0] = moved_first
-    new_second[0] = moved_second
-
-
-def adam_step(master, first, second, grad, slot_count, block_rows=ADAM_ROWS):
+        settle(arrive.at[k, 4], pools[k].at[pl.ds(0, 28)])
+        settle(send.at[k], meter.at[:, :, pl.ds(0, width)])
+    settle(n_send.at[0], count_g.at[pl.ds(0, 7)])
+    settle(n_send.at[1], count_x.at[pl.ds(0, 3)])
+    settle(n_send.at[2], count_z.at[pl.ds(0, 3)])
+
+
+def adam_kernel(block, slot_count, master, first, second, grad_ref, *refs):
+    outs, (grad, moved, in_sem, out_sem) = refs[:3], refs[3:]
+    blocks = range(grad.shape[1] // block)
+    loads, stores = [], []
+    for i in blocks:
+        rows = pl.ds(i * block, block)
+        loads.append(pltpu.make_async_copy(grad_ref.at[:, rows], grad.at[:, rows], in_sem.at[i]))
+        loads[i].start()
+    inverse = 1.0 / slot_count[0:1, 0:1]
+    for i in blocks:
+        rows = pl.ds(i * block, block)
+        loads[i].wait()
+        scaled = grad[0, rows].astype(jnp.float32) * inverse
+        moved_first = 0.9 * first[0, rows] + 0.1 * scaled
+        moved_second = 0.999 * second[0, rows] + 0.001 * scaled * scaled
+        scale = jnp.sqrt(moved_second * (1.0 / second_correction)) + 1e-08
+        step_dir = moved_first * (1.0 / first_correction) / scale
+        moved[1, rows] = moved_first
+        moved[2, rows] = moved_second
+        moved[0, rows] = master[0, rows] - 0.01 * (step_dir + 0.1 * master[0, rows])
+        for j in (1, 2, 0):
+            stores.append(pltpu.make_async_copy(moved.at[j, rows], outs[j].at[0, rows], out_sem.at[i, j]))
+            stores[-1].start()
+    for copy in stores:
+        copy.wait()
+
+
+def adam_step(master, first, second, grad, slot_count):
     _, rows, ff = grad.shape
-    tile = pl.BlockSpec((1, block_rows, ff), lambda i: (0, i, 0))
     state = jax.ShapeDtypeStruct((1, rows, ff), jnp.float32)
+    vmem, hbm = pl.BlockSpec(memory_space=pltpu.VMEM), pl.BlockSpec(memory_space=pl.ANY)
+    blocks = rows // ADAM_ROWS
     return pl.pallas_call(
-        adam_kernel,
+        functools.partial(adam_kernel, ADAM_ROWS),
         name="adam",
-        grid=(rows // block_rows,),
         out_shape=(state, state, state),
-        in_specs=[pl.BlockSpec((1, LANES), lambda i: (0, 0)), tile, tile, tile, tile],
-        out_specs=(tile, tile, tile),
+        in_specs=[vmem, vmem, vmem, vmem, hbm],
+        out_specs=(hbm, hbm, hbm),
+        scratch_shapes=[
+            pltpu.VMEM(grad.shape, grad.dtype),
+            pltpu.VMEM((3, rows, ff), jnp.float32),
+            pltpu.SemaphoreType.DMA((blocks,)),
+            pltpu.SemaphoreType.DMA((blocks, 3)),
+        ],
     )(slot_count, master, first, second, grad)
 
 
@@ -614,25 +623,25 @@
             + [pltpu.VMEM((4, 4, 2, rows, w), f32) for _, _, w in pieces]
             + tallies
             + [pltpu.VMEM((1, 1, experts), i32), pltpu.SMEM((8, experts), i32)]
-            + [dma((m,)), dma((m,)), dma((m,)), dma((m, 4)), dma((m, 4)), dma((m, 4)), dma((m, 4))]
-            + [dma((m, 8)), dma((m, 8)), dma((m,)), dma((14,)), dma((14,)), dma((3,))],
+            + [pltpu.VMEM((68 + 2 * l1 + 2 * l2, rows, max(w for _, _, w in pieces)), f32)]
+            + [dma((m,)), dma((m,)), dma((m, 5)), dma((3,)), dma((3,)), dma((3,))],
         )
         for number, (l1, l2) in enumerate(TIERS)
     ]
 
     old, new = old_owner.reshape(row), new_owner.reshape(row)
-    table = pl.pallas_call(
+    table, tally, tier = pl.pallas_call(
         plan_kernel,
         name="plan",
-        out_shape=jax.ShapeDtypeStruct((8, experts), i32),
-        in_specs=[vmem, vmem],
-        out_specs=vmem,
-    )(old, new)
+        out_shape=(jax.ShapeDtypeStruct((8, experts), i32), jax.ShapeDtypeStruct(row, i32), jax.ShapeDtypeStruct((1,), i32)),
+        in_specs=[vmem, vmem, vmem],
+        out_specs=(vmem, vmem, pl.BlockSpec(memory_space=pltpu.SMEM)),
+    )(old, new, counts.reshape(row))
     master, first, second, slot_count = lax.switch(
-        table[5, 0],
+        tier[0],
         branches + [spread],
         table,
-        counts.reshape(row),
+        tally,
         old,
         new,
         old_master,

time: 65 us -> 57.4 us (0.88)
  Pallas kernels: 61.4 us -> 54.3 us
  local copies, waits for them, and re-layouts: 1.83 us -> 0.66 us
    pallas_call x1, Pallas kernels: 56.8 us -> 49.8 us  [run(): pl.pallas_call(kernel, name=name, out_shape=(landed, landed, landed, jax....]
    unnamed x6 -> x4, local copies, waits for them, and re-layouts: 1.31 us -> 0.66 us
where the time goes in v4:
time: 57.4 us; the launch traced here: 56.7 us
  Pallas kernels  54.3 us (95%)
  between operations  1.49 us (3%)
  local copies, waits for them, and re-layouts  0.66 us (1%)
    pallas_call x1, Pallas kernels, run(): pl.pallas_call(kernel, name=name, out_shape=(landed, landed, landed, jax....  49.8 us
    pallas_call x1, Pallas kernels, adam_step(): pl.pallas_call(functools.partial(adam_kernel, ADAM_ROWS), name='adam', ou...  2.71 us
    pallas_call x1, Pallas kernels, body(): pl.pallas_call(plan_kernel, name='plan', out_shape=(jax.ShapeDtypeStruct(...  1.78 us

profile of v4, /device:TPU:1, one launch (start us, length us, event | category | flops | bytes accessed | tf_op | source)
XLA Modules:
  0.0 56.7 jit_solution(6115199076752879268)
XLA Ops:
  0.6 0.0 copy-start
  0.6 0.0 copy-start.1
  0.7 0.6 %copy-done = s32[128]{0:T(128)S(1)} copy-done((s32[128]{0:T(128)S(1)}, s32[128]{0:T(128)}, u32[]{:S(2)}) %copy-start) | copy-done | bytes 536
  1.3 0.0 copy-done.1
  1.3 1.8 %plan.1 = (s32[8,128]{1,0:T(8,128)S(1)}, s32[1,128]{1,0:T(1,128)S(1)}, s32[1]{0:T(128)}) custom-call(s32[1,128]{1,0:T(1,128)S(1)} %bitcast.10, s32[1,128]{1,0:T(1,128)S(1)} %bitcast.16, s32[1,128]{1,0:T(1,128)} %bitcast.22), custom_call_target="tpu_custom_call" | custom-call | tf_op jit(solution)/shard_map/plan/pallas_call | solution.py:633
  3.7 50.1 %conditional.1 = ((f32[4,4,8,1536]{3,2,1,0:T(8,128)S(1)}, f32[4,4,8,1536]{3,2,1,0:T(8,128)S(1)}, f32[4,4,8,1536]{3,2,1,0:T(8,128)S(1)}, f32[1,128]{1,0:T(1,128)S(1)})) conditional(s32[]{:T(128)} %bitcast.3, (s32[8,128]{1,0:T(8,128)S(1)}, s32[1,128]{1,0:T(1,128)S(1)}, s32[1,128]{1,0:T(1,128)S(1)}, ...), branch_computations={%region_0.0_spmd, %region_1.0_spmd, %region_2.0_spmd, %region_3.0_... | conditional | bytes 8 | solution.py:640
  3.8 49.8 %routed_16.1 = (f32[4,4,8,1536]{3,2,1,0:T(8,128)S(1)}, f32[4,4,8,1536]{3,2,1,0:T(8,128)S(1)}, f32[4,4,8,1536]{3,2,1,0:T(8,128)S(1)}, f32[1,128]{1,0:T(1,128)S(1)}) custom-call(s32[8,128]{1,0:T(8,128)S(1)} %get-tuple-element.98.table_ref, s32[1,128]{1,0:T(1,128)S(1)} %get-tuple-element.99.counts_ref, s32[1,128]{1,0:T(1,128)S(1)} %get-tuple-element.100.old_owner_ref, ...), custom_call_target="tpu_custom_call" | custom-call | tf_op jit(solution)/shard_map/cond/branch_0_fun/routed_16/pallas_call | solution.py:573
  53.8 2.7 %adam.1 = (f32[1,128,1536]{2,1,0:T(8,128)}, f32[1,128,1536]{2,1,0:T(8,128)}, f32[1,128,1536]{2,1,0:T(8,128)}) custom-call(f32[1,128]{1,0:T(1,128)S(1)} %get-tuple-element.177.slot_count, f32[1,128,1536]{2,1,0:T(8,128)S(1)} %bitcast.7, f32[1,128,1536]{2,1,0:T(8,128)S(1)} %bitcast.8, f32[1,128,1536]{2,1,0:T(8,128)S(1)} %bitcast.9, bf16[1,128,1536]{2,1,0:T(8,128)(2,1)} %grad_ref.1), custom_call_target="tpu_custom_call" | custom-call | tf_op jit(solution)/shard_map/adam/pallas_call | solution.py:546
Async XLA Ops:
  0.6 0.7 %copy-start = (s32[128]{0:T(128)S(1)}, s32[128]{0:T(128)}, u32[]{:S(2)}) copy-start(s32[128]{0:T(128)} %param.17) | copy-start | bytes 1540
  0.6 0.7 %copy-start.1 = (s32[128]{0:T(128)S(1)}, s32[128]{0:T(128)}, u32[]{:S(2)}) copy-start(s32[128]{0:T(128)} %param.18) | copy-start | bytes 1540

commit v5 on v4

--- a/solution.py
+++ b/solution.py
@@ -14,6 +14,8 @@
 Y_LAG = 4
 ADAM_ROWS = 16
 DEPTH = 4
+UNROLL = 2
+UNROLL_X = 2
 X_AFTER = 3
 Z_AFTER = 7
 TALLY = 2
@@ -33,7 +35,7 @@
 
 
 def exchange_kernel(
-    chunks, quarter, table_ref, counts_ref, old_owner_ref, new_owner_ref, *refs
+    chunks, quarter, table_ref, counts_ref, owners_ref, *refs
 ):
     states, (outs, slot_count_ref), scratch = refs[:3], (refs[3:6], refs[6]), refs[7:]
     n = len(chunks)
@@ -74,8 +76,7 @@
         return pl.ds(pl.multiple_of(owner_y * quarter + offset, LANES), width)
 
     small = [
-        pltpu.make_async_copy(old_owner_ref, owners.at[0], small_sem.at[0]),
-        pltpu.make_async_copy(new_owner_ref, owners.at[1], small_sem.at[1]),
+        pltpu.make_async_copy(owners_ref, owners, small_sem.at[0]),
         pltpu.make_async_copy(counts_ref, count_g.at[gx], small_sem.at[2]),
     ]
     for copy in small:
@@ -229,11 +230,19 @@
     return device(x, y, z, other)
 
 
-def plan_kernel(old_owner_ref, new_owner_ref, counts_ref, table_ref, tally_ref, tier_ref):
-    tally_ref[...] = counts_ref[...]
+def plan_kernel(old_owner_ref, new_owner_ref, counts_ref, table_ref, tally_ref, owners, sems):
+    loads = [
+        pltpu.make_async_copy(old_owner_ref, owners.at[0], sems.at[0]),
+        pltpu.make_async_copy(new_owner_ref, owners.at[1], sems.at[1]),
+        pltpu.make_async_copy(counts_ref, tally_ref, sems.at[2]),
+    ]
+    for copy in loads:
+        copy.start()
+    for copy in loads:
+        copy.wait()
     f32, i32 = jnp.float32, jnp.int32
     square, row = (LANES, LANES), (8, LANES)
-    old, new = (jnp.broadcast_to(ref[...], square) for ref in (old_owner_ref, new_owner_ref))
+    old, new = (jnp.broadcast_to(owners[i], square) for i in range(2))
     sub, lane = lax.broadcasted_iota(i32, square, 0), lax.broadcasted_iota(i32, square, 1)
 
     dest_down = jnp.sum(jnp.where(old == sub, new, 0).astype(f32), axis=1, keepdims=True)
@@ -326,8 +335,7 @@
     )
     places = lax.broadcasted_iota(i32, (32, LANES), 0)
     lanes = lax.broadcasted_iota(i32, (32, LANES), 1)
-    tier_ref[0] = jnp.max(tier.astype(f32)).astype(i32)
-    table = jnp.zeros((32, LANES), f32)
+    table = jnp.where(lanes == 5, tier[:1], 0).astype(f32)
     for k, (position, value) in enumerate(sends):
         hit = jnp.broadcast_to(position[:1], (32, LANES)) == places
         entry = jnp.sum(jnp.where(hit, value[:1], 0).astype(f32), axis=1, keepdims=True)
@@ -336,7 +344,7 @@
     table_ref[...] = table.T[:8].astype(i32)
 
 
-def routed_kernel(chunks, half, l1, l2, table_ref, counts_ref, old_owner_ref, new_owner_ref, *refs):
+def routed_kernel(chunks, half, l1, l2, table_ref, counts_ref, owners_ref, *refs):
     states, (outs, slot_count_ref), scratch = refs[:3], (refs[3:6], refs[6]), refs[7:]
     n = len(chunks)
     pools, landed, b1, b2, b3, held = (scratch[i * n : (i + 1) * n] for i in range(6))
@@ -357,7 +365,7 @@
         pl.semaphore_signal(barrier, inc=1, device_id=peer, device_id_type=MESH)
     small = [
         pltpu.make_async_copy(table_ref, plan, small_sem.at[0]),
-        pltpu.make_async_copy(new_owner_ref, owners.at[0], small_sem.at[1]),
+        pltpu.make_async_copy(owners_ref, owners, small_sem.at[1]),
         pltpu.make_async_copy(counts_ref, count_g.at[gx], small_sem.at[2]),
     ]
     for copy in small:
@@ -391,8 +399,6 @@
         )
     for copy in small:
         copy.wait()
-    for peer in gs[1:]:
-        remote(counts_ref, count_g.at[gx], n_send.at[0], n_recv.at[0], peer)
 
     def tally_x():
         settle(n_recv.at[0], count_g.at[pl.ds(0, 7)])
@@ -419,7 +425,7 @@
         return jnp.where(jnp.full(here.shape, entry, jnp.int32) < 32, here, arrived)
 
     def steps(size, place):
-        lax.fori_loop(0, size, place, 0, unroll=size if size % 2 else size // 2)
+        lax.fori_loop(0, size, place, 0, unroll=UNROLL)
 
     def first_round(k):
         own[k].wait()
@@ -462,7 +468,7 @@
                     b3[k][d - 1, to_z, to_c] = tile
                 return carry
 
-            lax.fori_loop(0, 8, place, 0, unroll=8)
+            lax.fori_loop(0, 8, place, 0, unroll=UNROLL_X)
         for d in ORDER:
             remote(b3[k].at[d - 1], held[k].at[x], send.at[k], arrive.at[k, 3], xs[d])
 
@@ -481,6 +487,8 @@
 
     for k in range(min(DEPTH, n)):
         first_round(k)
+    for peer in gs[1:]:
+        remote(counts_ref, count_g.at[gx], n_send.at[0], n_recv.at[0], peer)
     for i in range(n + Z_AFTER):
         if i < n:
             second_round(i)
@@ -500,7 +508,7 @@
             tally_send_z()
     settle(n_recv.at[2], count_z.at[pl.ds(0, 3)])
     totals = jnp.sum(count_z[...], axis=0)
-    mine = jnp.where(owners[0] == gx * 16 + gy, totals, 0.0)
+    mine = jnp.where(owners[1] == gx * 16 + gy, totals, 0.0)
     slot_count_ref[...] = jnp.broadcast_to(jnp.sum(mine, axis=1, keepdims=True), (1, LANES))
     for k, (_, _, width) in enumerate(chunks):
         own[k].wait()
@@ -574,7 +582,7 @@
                 kernel,
                 name=name,
                 out_shape=(landed, landed, landed, jax.ShapeDtypeStruct(row, f32)),
-                in_specs=[hbm] * 7,
+                in_specs=[hbm] * 6,
                 out_specs=(hbm, hbm, hbm, vmem),
                 scratch_shapes=scratch,
                 compiler_params=pltpu.CompilerParams(
@@ -622,28 +630,28 @@
             + [pltpu.VMEM((3, 4, 2, rows, w), f32) for _, _, w in pieces]
             + [pltpu.VMEM((4, 4, 2, rows, w), f32) for _, _, w in pieces]
             + tallies
-            + [pltpu.VMEM((1, 1, experts), i32), pltpu.SMEM((8, experts), i32)]
+            + [pltpu.VMEM((2, 1, experts), i32), pltpu.SMEM((8, experts), i32)]
             + [pltpu.VMEM((68 + 2 * l1 + 2 * l2, rows, max(w for _, _, w in pieces)), f32)]
             + [dma((m,)), dma((m,)), dma((m, 5)), dma((3,)), dma((3,)), dma((3,))],
         )
         for number, (l1, l2) in enumerate(TIERS)
     ]
 
-    old, new = old_owner.reshape(row), new_owner.reshape(row)
-    table, tally, tier = pl.pallas_call(
+    stay = pl.BlockSpec(memory_space=pltpu.HBM)
+    table, tally, owners = pl.pallas_call(
         plan_kernel,
         name="plan",
-        out_shape=(jax.ShapeDtypeStruct((8, experts), i32), jax.ShapeDtypeStruct(row, i32), jax.ShapeDtypeStruct((1,), i32)),
-        in_specs=[vmem, vmem, vmem],
-        out_specs=(vmem, vmem, pl.BlockSpec(memory_space=pltpu.SMEM)),
-    )(old, new, counts.reshape(row))
+        out_shape=(jax.ShapeDtypeStruct((8, experts), i32), jax.ShapeDtypeStruct(row, i32), jax.ShapeDtypeStruct((2, 1, experts), i32)),
+        in_specs=[stay, stay, stay],
+        out_specs=(vmem, vmem, vmem),
+        scratch_shapes=[dma((3,))],
+    )(old_owner.reshape(row), new_owner.reshape(row), counts.reshape(row))
     master, first, second, slot_count = lax.switch(
-        tier[0],
+        table[5, 0],
         branches + [spread],
         table,
         tally,
-        old,
-        new,
+        owners,
         old_master,
         old_first,
         old_second,

time: 57.4 us -> 57.1 us (level)
    pallas_call x1, Pallas kernels: 49.8 us -> 50.5 us  [run(): pl.pallas_call(kernel, name=name, out_shape=(landed, landed, landed, jax....]
    unnamed x4 -> x0, local copies, waits for them, and re-layouts: 0.66 us -> none
where the time goes in v5:
time: 57.1 us; the launch traced here: 56.9 us
  Pallas kernels  54.7 us (96%)
  between operations  1.48 us (3%)
    pallas_call x1, Pallas kernels, run(): pl.pallas_call(kernel, name=name, out_shape=(landed, landed, landed, jax....  50.5 us
    pallas_call x1, Pallas kernels, adam_step(): pl.pallas_call(functools.partial(adam_kernel, ADAM_ROWS), name='adam', ou...  2.71 us
    pallas_call x1, Pallas kernels, body(): pl.pallas_call(plan_kernel, name='plan', out_shape=(jax.ShapeDtypeStruct(...  1.46 us

profile of v5, /device:TPU:1, one launch (start us, length us, event | category | flops | bytes accessed | tf_op | source)
XLA Modules:
  0.0 56.9 jit_solution(17640517235917405421)
XLA Ops:
  0.6 1.5 %plan.1 = (s32[8,128]{1,0:T(8,128)S(1)}, s32[1,128]{1,0:T(1,128)S(1)}, s32[2,1,128]{2,1,0:T(1,128)S(1)}) custom-call(s32[1,128]{1,0:T(1,128)} %bitcast.10, s32[1,128]{1,0:T(1,128)} %bitcast.11, s32[1,128]{1,0:T(1,128)} %bitcast.12), custom_call_target="tpu_custom_call" | custom-call | tf_op jit(solution)/shard_map/plan/pallas_call | solution.py:641
  2.1 0.5 slice.3
  3.3 50.8 %conditional.1 = ((f32[4,4,8,1536]{3,2,1,0:T(8,128)S(1)}, f32[4,4,8,1536]{3,2,1,0:T(8,128)S(1)}, f32[4,4,8,1536]{3,2,1,0:T(8,128)S(1)}, f32[1,128]{1,0:T(1,128)S(1)})) conditional(s32[]{:T(128)} %bitcast.3, (s32[8,128]{1,0:T(8,128)S(1)}, s32[1,128]{1,0:T(1,128)S(1)}, s32[2,1,128]{2,1,0:T(1,128)S(1)}, ...), branch_computations={%region_0.0_spmd, %region_1.0_spmd, %region_2.0_spmd, %region_3.0_... | conditional | bytes 8 | solution.py:649
  3.3 50.5 %routed_17.1 = (f32[4,4,8,1536]{3,2,1,0:T(8,128)S(1)}, f32[4,4,8,1536]{3,2,1,0:T(8,128)S(1)}, f32[4,4,8,1536]{3,2,1,0:T(8,128)S(1)}, f32[1,128]{1,0:T(1,128)S(1)}) custom-call(s32[8,128]{1,0:T(8,128)S(1)} %get-tuple-element.94.table_ref, s32[1,128]{1,0:T(1,128)S(1)} %get-tuple-element.95.counts_ref, s32[2,1,128]{2,1,0:T(1,128)S(1)} %get-tuple-element.96.owners_ref, ...), custom_call_target="tpu_custom_call" | custom-call | tf_op jit(solution)/shard_map/cond/branch_1_fun/routed_17/pallas_call | solution.py:581
  54.0 2.7 %adam.1 = (f32[1,128,1536]{2,1,0:T(8,128)}, f32[1,128,1536]{2,1,0:T(8,128)}, f32[1,128,1536]{2,1,0:T(8,128)}) custom-call(f32[1,128]{1,0:T(1,128)S(1)} %get-tuple-element.162.slot_count, f32[1,128,1536]{2,1,0:T(8,128)S(1)} %bitcast.7, f32[1,128,1536]{2,1,0:T(8,128)S(1)} %bitcast.8, f32[1,128,1536]{2,1,0:T(8,128)S(1)} %bitcast.9, bf16[1,128,1536]{2,1,0:T(8,128)(2,1)} %grad_ref.1), custom_call_target="tpu_custom_call" | custom-call | tf_op jit(solution)/shard_map/adam/pallas_call | solution.py:554
